TPU v7x, 256 devices: a 2x2x32 block of a 4x8x32 slice. The times are simulated.
256 devices in a mesh: groups: 4 (over y, x), dp: 64 (over z, core).
Axes of the slice: x: 2, y: 2, z: 32, core: 2. Of those that a mesh axis runs over, the one named last changes fastest.
The devices are a block of a 4x8x32 slice.
Arguments:
- inputs: bfloat16 [2048, 32, 8192], P(('groups', 'dp')), parts along dimension 0, may hold values from -6 to 6
- out_grads: bfloat16 [2048, 32, 8192], P(('groups', 'dp')), parts along dimension 0, may hold values from -3 to 3
- token_ids: int32 [2048, 32], P(('groups', 'dp')), parts along dimension 0, may hold values from 0 to 128255
- in_signs: int32 [64, 8192], replicated, may hold values from 0 to 1
- out_signs: int32 [64, 8192], replicated, may hold values from 0 to 1
Outputs:
- fisher_block: bfloat16 [16384, 4096], P(('groups', 'dp')), parts along dimension 0
- precond_features: float32 [2048, 4096], P(('groups', 'dp')), parts along dimension 0
There are 4 independent parts, one for each index of `groups`. A program takes and returns all parts, laid end to end along the dimension named above; an argument that names none is the same for every part. Nothing has to cross between parts.
All inputs are finite; a program needn't handle non-finite values.
Results may differ from a plain program's by a relative error of at most 0.0057.
Values may be sent and summed in bfloat16 or wider, within the bound.
No kernel may reach another device: no remote copies, remote signals or barrier semaphores. Data moves between devices by JAX's collectives and lax.ppermute only.
A program may use at most 64 MiB of HBM per device.

v0:
```python
import jax
import jax.numpy as jnp
from jax import lax
from jax.sharding import PartitionSpec as P

RESERVED = 32064


def from_everyone(array, axis):
    devices = lax.axis_size(axis)
    return lax.all_to_all(
        jnp.broadcast_to(array[None], (devices, *array.shape)), axis, 0, 0, tiled=True
    )


def of_everyone(array, axis):
    return from_everyone(array, axis).sum(axis=0)


def project(values, sign_bits):
    sign_table = (2 * sign_bits - 1).astype(jnp.bfloat16)
    in_width = values.shape[-1]
    flat_rows = values.reshape(-1, in_width)
    product = lax.dot_general(
        flat_rows, sign_table, (((1,), (1,)), ((), ())), preferred_element_type=jnp.float32
    )
    return product * in_width ** (-0.5)


def on_device(inputs, out_grads, token_ids, in_signs, out_signs):
    local_count, length = token_ids.shape
    keep_mask = (token_ids >= RESERVED).astype(jnp.float32).reshape(-1, 1)
    in_proj = (project(inputs, in_signs) * keep_mask).reshape(local_count, length, -1)
    out_proj = project(out_grads, out_signs).reshape(local_count, length, -1)
    outer = jnp.einsum("sti,stj->sij", in_proj, out_proj, precision=lax.Precision.HIGHEST)
    per_sample = outer.reshape(local_count, -1).astype(jnp.bfloat16)
    features = per_sample.shape[1]
    devices = lax.axis_size("dp")
    own_rows = features // devices
    first_row = lax.axis_index("dp") * own_rows
    samples = local_count * devices
    own_squares = jnp.sum(jnp.square(per_sample.astype(jnp.float32)))
    trace_sum = of_everyone(own_squares, "dp")
    block_rows = lax.all_gather(per_sample, "dp", axis=0, tiled=True)
    columns = lax.dynamic_slice_in_dim(block_rows, first_row, own_rows, 1)
    fisher_part = lax.dot_general(
        columns, block_rows, (((0,), (0,)), ((), ())), preferred_element_type=jnp.float32
    )
    gathered = block_rows
    fisher_sum, gathered = (fisher_part, gathered)
    fisher_block = (fisher_sum / samples).astype(jnp.bfloat16)
    gram_full = lax.dot_general(
        gathered, gathered, (((1,), (1,)), ((), ())), preferred_element_type=jnp.float32
    )
    inverse_trace = features / trace_sum
    system = jnp.eye(samples, dtype=jnp.float32) + inverse_trace * gram_full
    factor = jnp.linalg.cholesky(system)
    positions = lax.broadcasted_iota(jnp.int32, (samples, local_count), 0)
    columns_index = lax.broadcasted_iota(jnp.int32, (samples, local_count), 1)
    selector = (positions == lax.axis_index("dp") * local_count + columns_index).astype(jnp.float32)
    picked = jax.scipy.linalg.cho_solve((factor, True), selector)
    precond_features = jnp.dot(
        picked.T, gathered, precision=lax.Precision.HIGHEST, preferred_element_type=jnp.float32
    )
    return (fisher_block, precond_features)


def solution(mesh):
    in_specs = (
        P(("groups", "dp"), None, None),
        P(("groups", "dp"), None, None),
        P(("groups", "dp"), None),
        P(),
        P(),
    )
    out_specs = (P(("groups", "dp"), None), P(("groups", "dp"), None))
    return jax.shard_map(
        on_device, mesh=mesh, in_specs=in_specs, out_specs=out_specs, check_vma=False
    )
```

profile of v0, /device:TPU:37, one launch (start us, length us, event | category | flops | bytes accessed | tf_op | source)
XLA Modules:
  0.0 320.2 jit_solution(13530040438665092314)
XLA Ops:
  7.3 0.8 compare_select_fusion
  8.2 4.2 %fusion.2 = f32[256,64]{0,1:T(8,128)S(1)} fusion(bf16[256,8192]{1,0:T(8,128)(2,1)} %bitcast.76, s32[64,8192]{1,0:T(8,128)} %param.8, f32[256]{0:T(256)S(1)} %mul.49), kind=kOutput, calls=%fused_computation.16 | convolution fusion | flops 270024704 | bytes 6358016 | tf_op jit(solution)/shard_map/dot_general | solution.py:24
  12.5 3.6 %fusion.1 = f32[256,64]{0,1:T(8,128)S(1)} fusion(bf16[256,8192]{1,0:T(8,128)(2,1)} %bitcast.75, s32[64,8192]{1,0:T(8,128)S(1)} %copy-done.1), kind=kOutput, calls=%fused_computation.14 | convolution fusion | flops 270024704 | bytes 6356992 | tf_op jit(solution)/shard_map/dot_general | solution.py:24
  16.2 1.2 multiply_reduce_fusion
  17.4 0.8 convert_element_type.33
  18.3 1.2 broadcast_in_dim.3
  19.5 34.5 %all-to-all-start = ((f32[64,1,1]{2,1,0:T(1,128)}), f32[64,1,1]{2,1,0:T(1,128)S(1)}, u32[]{:S(2)}, u32[]{:S(2)}) async-start(f32[64,1,1]{2,1,0:T(1,128)} %broadcast_in_dim.3), calls=%async_computation | async-start | bytes 65536 | tf_op jit(solution)/shard_map/all_to_all | solution.py:11
  54.1 21.8 %all-to-all-done = f32[64,1,1]{2,1,0:T(1,128)S(1)} async-done(((f32[64,1,1]{2,1,0:T(1,128)}), f32[64,1,1]{2,1,0:T(1,128)S(1)}, u32[]{:S(2)}, u32[]{:S(2)}) %all-to-all-start) | async-done | bytes 288 | tf_op jit(solution)/shard_map/all_to_all | solution.py:11
  76.0 0.7 reduce_sum.19
  77.3 88.8 %all-gather.2.cloned.1.call-done = bf16[512,4096]{1,0:T(8,128)(2,1)} async-done(((bf16[8,4096]{1,0:T(8,128)(2,1)}), bf16[512,4096]{1,0:T(8,128)(2,1)}) %all-gather.2.cloned.1.call-update) | async-done | bytes 4194320 | tf_op jit(solution)/shard_map/all_gather | solution.py:44
  166.2 5.8 %convert_add_fusion = (f32[512,512]{0,1:T(8,128)S(1)}, f32[512,512]{0,1:T(8,128)S(1)}) fusion(bf16[512,4096]{1,0:T(8,128)(2,1)} %all-gather.2.cloned.1.call-done, f32[]{:T(128)S(6)} %div.19), kind=kOutput, calls=%fused_computation.28 | convolution fusion | flops 2148532224 | bytes 6291460 | tf_op jit(solution)/shard_map/dot_general | solution.py:52
  172.6 11.7 %cholesky.104 = f32[128,128]{1,0:T(8,128)S(1)} custom-call(f32[128,128]{1,0:T(8,128)S(1)} %cholesky.266), custom_call_target="Cholesky" | custom-call | tf_op jit(solution)/shard_map/jit(cholesky)/cholesky | solution.py:57
  184.4 9.8 %custom-call.34 = f32[1,128,128]{1,2,0:T(8,128)S(1)} custom-call(f32[1,128,128]{2,1,0:T(8,128)S(1)} %get-tuple-element.29), custom_call_target="InvertDiagBlocksLowerTriangular" | custom-call | tf_op jit(solution)/shard_map/jit(cholesky)/cholesky | solution.py:57
  194.9 11.9 %cholesky.217 = f32[128,128]{1,0:T(8,128)S(1)} custom-call(f32[128,128]{1,0:T(8,128)S(1)} %cholesky.270), custom_call_target="Cholesky" | custom-call | tf_op jit(solution)/shard_map/jit(cholesky)/cholesky | solution.py:57
  206.9 9.8 %custom-call.35 = f32[1,128,128]{1,2,0:T(8,128)S(1)} custom-call(f32[1,128,128]{2,1,0:T(8,128)S(1)} %get-tuple-element.26), custom_call_target="InvertDiagBlocksLowerTriangular" | custom-call | tf_op jit(solution)/shard_map/jit(cholesky)/cholesky | solution.py:57
  217.4 11.7 %cholesky.238 = f32[128,128]{1,0:T(8,128)S(1)} custom-call(f32[128,128]{1,0:T(8,128)S(1)} %cholesky.275), custom_call_target="Cholesky" | custom-call | tf_op jit(solution)/shard_map/jit(cholesky)/cholesky | solution.py:57
  229.1 0.7 compare_reduce_fusion.1
  229.8 9.8 %custom-call.36 = f32[1,128,128]{1,2,0:T(8,128)S(1)} custom-call(f32[1,128,128]{2,1,0:T(8,128)S(1)} %get-tuple-element.23), custom_call_target="InvertDiagBlocksLowerTriangular" | custom-call | tf_op jit(solution)/shard_map/jit(cholesky)/cholesky | solution.py:57
  240.2 11.9 %cholesky.255 = f32[128,128]{1,0:T(8,128)S(1)} custom-call(f32[128,128]{1,0:T(8,128)S(1)} %convolution_subtract_fusion.2), custom_call_target="Cholesky" | custom-call | tf_op jit(solution)/shard_map/jit(cholesky)/cholesky | solution.py:57
  252.2 0.7 compare_reduce_fusion
  252.9 0.6 compare_reduce_fusion.2
  256.3 8.0 %while.1 = (s32[]{:T(128)}, f32[512,512]{1,0:T(8,128)S(1)}, s32[4,2]{0,1:T(2,128)S(1)}, f32[4,128,128]{2,1,0:T(8,128)S(1)}, s32[]{:T(128)}) while((s32[]{:T(128)}, f32[512,512]{1,0:T(8,128)S(1)}, s32[4,2]{0,1:T(2,128)S(1)}, f32[4,128,128]{2,1,0:T(8,128)S(1)}, s32[]{:T(128)}) %tuple.34), condition=%wide.while_cond, body=%wide.while_body.sunk | while | flops 2 | bytes 131181 | solution.py:61
  256.4 0.5 fusion.91
  256.9 1.4 bitcast_dynamic-update-slice_fusion.2
  258.4 0.5 fusion.91
  258.9 1.4 bitcast_dynamic-update-slice_fusion.2
  260.4 0.5 fusion.91
  260.9 1.4 bitcast_dynamic-update-slice_fusion.2
  262.9 1.4 bitcast_dynamic-update-slice_fusion.2
  264.3 39.3 %custom-call.37 = f32[4,128,128]{1,2,0:T(8,128)S(1)} custom-call(f32[4,128,128]{2,1,0:T(8,128)S(1)} %get-tuple-element.9), custom_call_target="InvertDiagBlocksLowerTriangular" | custom-call | tf_op jit(solution)/shard_map/jit(_cho_solve)/triangular_solve | solution.py:61
  306.5 4.6 %fusion.35 = f32[8,4096]{1,0:T(8,128)} fusion(bf16[512,4096]{1,0:T(8,128)(2,1)} %all-gather.2.cloned.1.call-done, f32[128,8]{0,1:T(8,128)S(1)} %fusion.33, f32[128,8]{0,1:T(8,128)S(1)} %fusion.31, f32[128,8]{0,1:T(8,128)S(1)} %fusion.29, f32[128,8]{0,1:T(8,128)S(1)} %fusion.27), kind=kOutput, calls=%fused_computation.75 | convolution fusion | flops 201338880 | bytes 4341760 | tf_op jit(solution)/shard_map/dot_general | solution.py:62
  311.2 1.7 fusion
  (50 shorter events, 7.0 us)
Async XLA Ops:
  7.2 5.3 %copy-start.1 = (s32[64,8192]{1,0:T(8,128)S(1)}, s32[64,8192]{1,0:T(8,128)}, u32[]{:S(2)}) copy-start(s32[64,8192]{1,0:T(8,128)} %param.9) | copy-start | bytes 6291460
  7.2 159.0 %all-gather.2.cloned.1.call-start = ((), (), s32[]{:S(2)}) async-start(), calls=%async_computation.1 | async-start | bytes 4259840 | tf_op jit(solution)/shard_map/all_gather | solution.py:44
  19.5 56.4 %all-to-all-start = ((f32[64,1,1]{2,1,0:T(1,128)}), f32[64,1,1]{2,1,0:T(1,128)S(1)}, u32[]{:S(2)}, u32[]{:S(2)}) async-start(f32[64,1,1]{2,1,0:T(1,128)} %broadcast_in_dim.3), calls=%async_computation | async-start | bytes 65536 | tf_op jit(solution)/shard_map/all_to_all | solution.py:11
  303.6 7.5 %copy-start = (bf16[512,4096]{1,0:T(8,128)(2,1)S(1)}, bf16[512,4096]{1,0:T(8,128)(2,1)}, u32[]{:S(2)}) copy-start(bf16[512,4096]{1,0:T(8,128)(2,1)} %all-gather.2.cloned.1.call-done) | copy-start | bytes 12582916
Sparse Core Ops, SparseCore 0:
  18.4 147.7 all-gather.1
where the time goes:
time: 324 us; the launch traced here: 320 us
  other arithmetic  120 us (37%)
  waiting for transfers between devices  111 us (34%)
  starting transfers between devices  34.6 us (11%)
  matrix products  26 us (8%)
  between operations  18 us (6%)
  local copies, waits for them, and re-layouts  10.7 us (3%)
    all_gather x1, waiting for transfers between devices, on_device(): block_rows = lax.all_gather(per_sample, 'dp', axis=0, tiled=True)  88.8 us
    another operation x14, other arithmetic, on_device(): factor = jnp.linalg.cholesky(system)  78.9 us
    another operation x3, other arithmetic, on_device(): picked = jax.scipy.linalg.cho_solve((factor, True), selector)  39.4 us
    all_to_all x1, starting transfers between devices, from_everyone(): lax.all_to_all(jnp.broadcast_to(array[None], (devices, *array.shape)), ax...  34.5 us
    all_to_all x1, waiting for transfers between devices, from_everyone(): lax.all_to_all(jnp.broadcast_to(array[None], (devices, *array.shape)), ax...  21.8 us
    another operation x12, local copies, waits for them, and re-layouts  7.92 us
    dot_general x2, matrix products, project(): lax.dot_general(flat_rows, sign_table, (((1,), (1,)), ((), ())), preferre...  7.8 us
  transfers between devices with their start and end apart: 2, of which 2 were waited for; matrix products, arithmetic and copies ran while one was open for 1% of the time, Pallas kernels for 0%

commit v1 on v0

v1 whole, which is shorter than its diff:
```python
import functools

import jax
import jax.numpy as jnp
from jax import lax
from jax.experimental import pallas as pl
from jax.experimental.pallas import tpu as pltpu
from jax.sharding import PartitionSpec as P

RESERVED = 32064
TOLERANCE = 1e-5


def project(values, sign_bits):
    sign_table = (2 * sign_bits - 1).astype(jnp.bfloat16)
    in_width = values.shape[-1]
    flat_rows = values.reshape(-1, in_width)
    product = lax.dot_general(
        flat_rows, sign_table, (((1,), (1,)), ((), ())), preferred_element_type=jnp.float32
    )
    return product * in_width ** (-0.5)


def gather_samples(own, axis):
    chips = lax.axis_size(axis) // 2
    turn = [(2 * z + c, 2 * z + 1 - c) for z in range(chips) for c in range(2)]

    def along(value, hops):
        pairs = [(2 * z, 2 * ((z + hops) % chips)) for z in range(chips)]
        pairs += [(2 * z + 1, 2 * ((z - hops) % chips) + 1) for z in range(chips)]
        return lax.ppermute(value, axis, pairs)

    carried = [own, lax.ppermute(own, axis, turn)]
    held = [own]
    far = chips // 2
    for distance in range(0, far, 2):
        last = distance + 2 == far
        onward = [along(value, 2) for value in (carried[:1] if last else carried)]
        held += [along(value, 1) for value in carried]
        held += onward
        carried = onward
    half = jnp.concatenate(held, axis=0)
    return jnp.concatenate([half, lax.ppermute(half, axis, turn)], axis=0)


def split3(value):
    high = value.astype(jnp.bfloat16)
    rest = value - high.astype(jnp.float32)
    mid = rest.astype(jnp.bfloat16)
    low = (rest - mid.astype(jnp.float32)).astype(jnp.bfloat16)
    return high, mid, low


def stack3(value):
    parts = [part.astype(jnp.float32) for part in split3(value)]
    return jnp.concatenate([*parts, jnp.zeros_like(value)], axis=0).astype(jnp.bfloat16)


def dot(left, right, dims=(1, 0)):
    return lax.dot_general(
        left, right, (((dims[0],), (dims[1],)), ((), ())), preferred_element_type=jnp.float32
    )


def tail_kernel(place_ref, all_ref, fisher_ref, precond_ref, columns_ref, high_ref, mid_ref, low_ref):
    samples, features = all_ref.shape
    own_rows = fisher_ref.shape[0]
    count = precond_ref.shape[0]
    gram = dot(all_ref[...], all_ref[...], (1, 1))
    row = lax.broadcasted_iota(jnp.int32, gram.shape, 0)
    column = lax.broadcasted_iota(jnp.int32, gram.shape, 1)
    on_diagonal = row == column
    diagonal = jnp.where(on_diagonal, gram, 0.0)
    across = jnp.sum(diagonal, axis=0, keepdims=True)
    down = jnp.sum(diagonal, axis=1, keepdims=True)
    factor = features / jnp.sum(across)
    across = lax.rsqrt(1.0 + factor * across)
    down = lax.rsqrt(1.0 + factor * down)
    system = (jnp.where(on_diagonal, 1.0, 0.0) + factor * gram) * (down * across)
    high_ref[...], mid_ref[...], low_ref[...] = split3(system)

    def apply(rows):
        stacked = stack3(rows)
        by_high = dot(stacked, high_ref[...])
        by_mid = dot(stacked[: 2 * count], mid_ref[...])
        by_low = dot(stacked[: 2 * count], low_ref[...])
        small = by_low[:count] + by_mid[count:] + by_high[2 * count : 3 * count]
        return by_high[:count] + (by_mid[:count] + by_high[count : 2 * count] + small)

    unit_row = lax.broadcasted_iota(jnp.int32, (count, samples), 0)
    unit_column = lax.broadcasted_iota(jnp.int32, (count, samples), 1)
    right = jnp.where(unit_row == unit_column, across, 0.0)
    start = jnp.sum(right * right, axis=1, keepdims=True)
    limit = TOLERANCE * TOLERANCE * start

    def step(solved, residual, direction, squares):
        image = apply(direction)
        curvature = jnp.sum(direction * image, axis=1, keepdims=True)
        length = squares / jnp.maximum(curvature, 1e-37)
        solved = solved + length * direction
        residual = residual - length * image
        new_squares = jnp.sum(residual * residual, axis=1, keepdims=True)
        direction = residual + (new_squares / jnp.maximum(squares, 1e-37)) * direction
        return solved, residual, direction, new_squares

    def unfinished(carry):
        index, open_rows, *_ = carry
        return jnp.logical_and(index < 4 * samples, open_rows > 0.0)

    def body(carry):
        index, _, *state = carry
        for _ in range(2):
            state = step(*state)
        open_rows = jnp.max(jnp.where(state[3] > limit, 1.0, 0.0))
        return (index + 2, open_rows, *state)

    first = (jnp.int32(0), jnp.float32(1.0), jnp.zeros_like(right), right, right, start)
    solved = lax.while_loop(unfinished, body, first)[2]

    place = place_ref[0]
    lanes = columns_ref.shape[0]
    block = pl.multiple_of((place * own_rows // lanes) * lanes, lanes)
    columns_ref[...] = all_ref[:, pl.ds(block, lanes)].astype(jnp.float32).T
    inside = pl.multiple_of(place * own_rows % lanes, own_rows)
    columns = columns_ref[pl.ds(inside, own_rows), :].astype(jnp.bfloat16)
    both = dot(jnp.concatenate([columns, stack3(solved * across)], axis=0), all_ref[...])
    fisher_ref[...] = (both[:own_rows] * (1.0 / samples)).astype(jnp.bfloat16)
    low, mid, high = (both[own_rows + k * count : own_rows + (k + 1) * count] for k in (2, 1, 0))
    precond_ref[...] = high + (mid + low)


def tail(gathered, place, count, own_rows):
    samples, features = gathered.shape
    vmem = pl.BlockSpec(memory_space=pltpu.VMEM)
    return pl.pallas_call(
        tail_kernel,
        name="fisher_and_solve",
        out_shape=(
            jax.ShapeDtypeStruct((own_rows, features), jnp.bfloat16),
            jax.ShapeDtypeStruct((count, features), jnp.float32),
        ),
        in_specs=[pl.BlockSpec(memory_space=pltpu.SMEM), vmem],
        out_specs=(vmem, vmem),
        scratch_shapes=[
            pltpu.VMEM((128, samples), jnp.float32),
            *[pltpu.VMEM((samples, samples), jnp.bfloat16)] * 3,
        ],
    )(place, gathered)


def on_device(inputs, out_grads, token_ids, in_signs, out_signs):
    local_count, length = token_ids.shape
    keep_mask = (token_ids >= RESERVED).astype(jnp.float32).reshape(-1, 1)
    in_proj = (project(inputs, in_signs) * keep_mask).reshape(local_count, length, -1)
    out_proj = project(out_grads, out_signs).reshape(local_count, length, -1)
    outer = jnp.einsum("sti,stj->sij", in_proj, out_proj, precision=lax.Precision.HIGHEST)
    per_sample = outer.reshape(local_count, -1).astype(jnp.bfloat16)
    gathered = gather_samples(per_sample, "dp")
    own_rows = per_sample.shape[1] // lax.axis_size("dp")
    place = lax.axis_index("dp").astype(jnp.int32).reshape(1)
    return tail(gathered, place, local_count, own_rows)


def solution(mesh):
    in_specs = (
        P(("groups", "dp"), None, None),
        P(("groups", "dp"), None, None),
        P(("groups", "dp"), None),
        P(),
        P(),
    )
    out_specs = (P(("groups", "dp"), None), P(("groups", "dp"), None))
    return jax.shard_map(
        on_device, mesh=mesh, in_specs=in_specs, out_specs=out_specs, check_vma=False
    )
```

time: 324 us -> 129 us (0.40); the launches traced: 320 us -> 129 us
  other arithmetic: 120 us -> 0.69 us
  waiting for transfers between devices: 111 us -> 4.9 us
  starting transfers between devices: 34.6 us -> 70.9 us
  Pallas kernels: 0 us -> 20.7 us
  matrix products: 26 us -> 8.58 us
  between operations: 18 us -> 0.72 us
  local copies, waits for them, and re-layouts: 10.7 us -> 22.7 us
    another operation x17 -> x0, other arithmetic: 118 us -> none  [the longest x14 78.9 us: on_device(): factor = jnp.linalg.cholesky(system)]
    all_gather x1 -> x0, waiting for transfers between devices: 88.8 us -> none  [on_device(): block_rows = lax.all_gather(per_sample, 'dp', axis=0, tiled=True)]
    ppermute x0 -> x33, starting transfers between devices: none -> 70.9 us  [the longest x31 60.2 us: along(): return lax.ppermute(value, axis, pairs)]
    all_to_all x1 -> x0, starting transfers between devices: 34.5 us -> none  [from_everyone(): lax.all_to_all(jnp.broadcast_to(array[None], (devices, *array.shape)), ax...]
    all_to_all x1 -> x0, waiting for transfers between devices: 21.8 us -> none  [from_everyone(): lax.all_to_all(jnp.broadcast_to(array[None], (devices, *array.shape)), ax...]
    pallas_call x0 -> x1, Pallas kernels: none -> 20.7 us  [tail(): pl.pallas_call(tail_kernel, name='fisher_and_solve', out_shape=(jax.Shape...]
    unnamed x4 -> x33, local copies, waits for them, and re-layouts: 0.01 us -> 20.1 us
    dot_general x3 -> x0, matrix products: 12.2 us -> none  [the longest x1 5.83 us: on_device(): lax.dot_general(gathered, gathered, (((1,), (1,)), ((), ())), preferred_e...]
  transfers between devices with their start and end apart: 2 -> 33, of which waited for: 2 -> 3; matrix products, arithmetic and copies ran while one was open for 1% -> 16% of each run, Pallas kernels for 0% -> 0%
where the time goes in v1:
time: 129 us
  starting transfers between devices  70.9 us (55%)
  local copies, waits for them, and re-layouts  22.7 us (18%)
  Pallas kernels  20.7 us (16%)
  matrix products  8.58 us (7%)
  waiting for transfers between devices  4.9 us (4%)
    ppermute x31, starting transfers between devices, along(): return lax.ppermute(value, axis, pairs)  60.2 us
    pallas_call x1, Pallas kernels, tail(): pl.pallas_call(tail_kernel, name='fisher_and_solve', out_shape=(jax.Shape...  20.7 us
    unnamed x33, local copies, waits for them, and re-layouts  20.1 us
    ppermute x1, starting transfers between devices, gather_samples(): return jnp.concatenate([half, lax.ppermute(half, axis, turn)], axis=0)  10.7 us
    dot_general x2, matrix products, project(): lax.dot_general(flat_rows, sign_table, (((1,), (1,)), ((), ())), preferre...  7.95 us
    ppermute x1, waiting for transfers between devices, gather_samples(): return jnp.concatenate([half, lax.ppermute(half, axis, turn)], axis=0)  4 us
  transfers between devices with their start and end apart: 33, of which 3 were waited for; matrix products, arithmetic and copies ran while one was open for 16% of the time, Pallas kernels for 0%

profile of v1, /device:TPU:37, one launch (start us, length us, event | category | flops | bytes accessed | tf_op | source)
XLA Modules:
  0.0 129.2 jit_solution(16369050249947863535)
XLA Ops:
  0.6 0.7 compare_select_fusion
  1.4 4.4 %fusion.1 = f32[256,64]{0,1:T(8,128)S(1)} fusion(bf16[256,8192]{1,0:T(8,128)(2,1)} %bitcast.14, s32[64,8192]{1,0:T(8,128)} %param.8, f32[256]{0:T(256)S(1)} %mul.33), kind=kOutput, calls=%fused_computation.6 | convolution fusion | flops 270024704 | bytes 6358016 | tf_op jit(solution)/shard_map/dot_general | solution.py:18
  5.9 3.6 %fusion = f32[256,64]{0,1:T(8,128)S(1)} fusion(bf16[256,8192]{1,0:T(8,128)(2,1)} %bitcast.13, s32[64,8192]{1,0:T(8,128)S(1)} %copy-done), kind=kOutput, calls=%fused_computation.4 | convolution fusion | flops 270024704 | bytes 6356992 | tf_op jit(solution)/shard_map/dot_general | solution.py:18
  10.4 23.7 %collective-permute-start = (bf16[8,4096]{1,0:T(8,128)(2,1)S(1)}, bf16[8,4096]{1,0:T(8,128)(2,1)S(1)}, u32[]{:S(2)}, u32[]{:S(2)}) collective-permute-start(bf16[8,4096]{1,0:T(8,128)(2,1)S(1)} %convert_element_type.16), channel_id=1, source_target_pairs={{0,2},{2,4},{4,6},{6,8},{8,10},{10,12},{12,14},{14,16},{16,18},{18... | collective-permute-start | bytes 196616 | tf_op jit(solution)/shard_map/ppermute | solution.py:31
  34.1 2.1 %collective-permute-start.3 = (bf16[8,4096]{1,0:T(8,128)(2,1)S(1)}, bf16[8,4096]{1,0:T(8,128)(2,1)S(1)}, u32[]{:S(2)}, u32[]{:S(2)}) collective-permute-start(bf16[8,4096]{1,0:T(8,128)(2,1)S(1)} %convert_element_type.16), channel_id=1, source_target_pairs={{0,4},{2,6},{4,8},{6,10},{8,12},{10,14},{12,16},{14,18},{16,20},{1... | collective-permute-start | bytes 196616 | tf_op jit(solution)/shard_map/ppermute | solution.py:31
  37.3 2.0 %collective-permute-start.4 = (bf16[8,4096]{1,0:T(8,128)(2,1)S(1)}, bf16[8,4096]{1,0:T(8,128)(2,1)S(1)}, u32[]{:S(2)}, u32[]{:S(2)}) collective-permute-start(bf16[8,4096]{1,0:T(8,128)(2,1)S(1)} %collective-permute-done.1), channel_id=1, source_target_pairs={{0,4},{2,6},{4,8},{6,10},{8,12},{10,14},{12,16},{14,18},{16,20},{1... | collective-permute-start | bytes 196616 | tf_op jit(solution)/shard_map/ppermute | solution.py:31
  39.3 1.4 %collective-permute-start.5 = (bf16[8,4096]{1,0:T(8,128)(2,1)S(1)}, bf16[8,4096]{1,0:T(8,128)(2,1)S(1)}, u32[]{:S(2)}, u32[]{:S(2)}) collective-permute-start(bf16[8,4096]{1,0:T(8,128)(2,1)S(1)} %collective-permute-done.3), channel_id=1, source_target_pairs={{0,2},{2,4},{4,6},{6,8},{8,10},{10,12},{12,14},{14,16},{16,18},{18... | collective-permute-start | bytes 196616 | tf_op jit(solution)/shard_map/ppermute | solution.py:31
  40.8 0.7 collective-permute-start.7
  42.1 1.0 collective-permute-start.6
  43.1 2.0 %collective-permute-start.8 = (bf16[8,4096]{1,0:T(8,128)(2,1)S(1)}, bf16[8,4096]{1,0:T(8,128)(2,1)S(1)}, u32[]{:S(2)}, u32[]{:S(2)}) collective-permute-start(bf16[8,4096]{1,0:T(8,128)(2,1)S(1)} %collective-permute-done.4), channel_id=1, source_target_pairs={{0,4},{2,6},{4,8},{6,10},{8,12},{10,14},{12,16},{14,18},{16,20},{1... | collective-permute-start | bytes 196616 | tf_op jit(solution)/shard_map/ppermute | solution.py:31
  45.5 1.5 %collective-permute-start.9 = (bf16[8,4096]{1,0:T(8,128)(2,1)S(1)}, bf16[8,4096]{1,0:T(8,128)(2,1)S(1)}, u32[]{:S(2)}, u32[]{:S(2)}) collective-permute-start(bf16[8,4096]{1,0:T(8,128)(2,1)S(1)} %collective-permute-done.7), channel_id=1, source_target_pairs={{0,2},{2,4},{4,6},{6,8},{8,10},{10,12},{12,14},{14,16},{16,18},{18... | collective-permute-start | bytes 196616 | tf_op jit(solution)/shard_map/ppermute | solution.py:31
  47.0 0.8 collective-permute-start.11
  50.4 1.4 %collective-permute-start.10 = (bf16[8,4096]{1,0:T(8,128)(2,1)S(1)}, bf16[8,4096]{1,0:T(8,128)(2,1)S(1)}, u32[]{:S(2)}, u32[]{:S(2)}) collective-permute-start(bf16[8,4096]{1,0:T(8,128)(2,1)S(1)} %collective-permute-done.8), channel_id=1, source_target_pairs={{0,2},{2,4},{4,6},{6,8},{8,10},{10,12},{12,14},{14,16},{16,18},{18... | collective-permute-start | bytes 196616 | tf_op jit(solution)/shard_map/ppermute | solution.py:31
  51.9 1.8 %collective-permute-start.12 = (bf16[8,4096]{1,0:T(8,128)(2,1)S(1)}, bf16[8,4096]{1,0:T(8,128)(2,1)S(1)}, u32[]{:S(2)}, u32[]{:S(2)}) collective-permute-start(bf16[8,4096]{1,0:T(8,128)(2,1)S(1)} %collective-permute-done.8), channel_id=1, source_target_pairs={{0,4},{2,6},{4,8},{6,10},{8,12},{10,14},{12,16},{14,18},{16,20},{1... | collective-permute-start | bytes 196616 | tf_op jit(solution)/shard_map/ppermute | solution.py:31
  53.8 1.6 %collective-permute-start.15 = (bf16[8,4096]{1,0:T(8,128)(2,1)S(1)}, bf16[8,4096]{1,0:T(8,128)(2,1)S(1)}, u32[]{:S(2)}, u32[]{:S(2)}) collective-permute-start(bf16[8,4096]{1,0:T(8,128)(2,1)S(1)} %collective-permute-done.11), channel_id=1, source_target_pairs={{0,4},{2,6},{4,8},{6,10},{8,12},{10,14},{12,16},{14,18},{16,20},{1... | collective-permute-start | bytes 196616 | tf_op jit(solution)/shard_map/ppermute | solution.py:31
  58.0 1.3 %collective-permute-start.14 = (bf16[8,4096]{1,0:T(8,128)(2,1)S(1)}, bf16[8,4096]{1,0:T(8,128)(2,1)S(1)}, u32[]{:S(2)}, u32[]{:S(2)}) collective-permute-start(bf16[8,4096]{1,0:T(8,128)(2,1)S(1)} %collective-permute-done.12), channel_id=1, source_target_pairs={{0,2},{2,4},{4,6},{6,8},{8,10},{10,12},{12,14},{14,16},{16,18},{18... | collective-permute-start | bytes 196616 | tf_op jit(solution)/shard_map/ppermute | solution.py:31
  59.3 0.9 collective-permute-start.16
  60.2 0.8 collective-permute-start.17
  61.0 1.6 %collective-permute-start.19 = (bf16[8,4096]{1,0:T(8,128)(2,1)S(1)}, bf16[8,4096]{1,0:T(8,128)(2,1)S(1)}, u32[]{:S(2)}, u32[]{:S(2)}) collective-permute-start(bf16[8,4096]{1,0:T(8,128)(2,1)S(1)} %collective-permute-done.15), channel_id=1, source_target_pairs={{0,4},{2,6},{4,8},{6,10},{8,12},{10,14},{12,16},{14,18},{16,20},{1... | collective-permute-start | bytes 196616 | tf_op jit(solution)/shard_map/ppermute | solution.py:31
  65.9 1.9 %collective-permute-start.20 = (bf16[8,4096]{1,0:T(8,128)(2,1)S(1)}, bf16[8,4096]{1,0:T(8,128)(2,1)S(1)}, u32[]{:S(2)}, u32[]{:S(2)}) collective-permute-start(bf16[8,4096]{1,0:T(8,128)(2,1)S(1)} %collective-permute-done.16), channel_id=1, source_target_pairs={{0,4},{2,6},{4,8},{6,10},{8,12},{10,14},{12,16},{14,18},{16,20},{1... | collective-permute-start | bytes 196616 | tf_op jit(solution)/shard_map/ppermute | solution.py:31
  68.2 1.2 collective-permute-start.23
  72.5 1.2 collective-permute-start.24
  73.7 1.4 %collective-permute-start.25 = (bf16[8,4096]{1,0:T(8,128)(2,1)S(1)}, bf16[8,4096]{1,0:T(8,128)(2,1)S(1)}, u32[]{:S(2)}, u32[]{:S(2)}) collective-permute-start(bf16[8,4096]{1,0:T(8,128)(2,1)S(1)} %collective-permute-done.23), channel_id=1, source_target_pairs={{0,2},{2,4},{4,6},{6,8},{8,10},{10,12},{12,14},{14,16},{16,18},{18... | collective-permute-start | bytes 196616 | tf_op jit(solution)/shard_map/ppermute | solution.py:31
  75.1 1.9 %collective-permute-start.27 = (bf16[8,4096]{1,0:T(8,128)(2,1)S(1)}, bf16[8,4096]{1,0:T(8,128)(2,1)S(1)}, u32[]{:S(2)}, u32[]{:S(2)}) collective-permute-start(bf16[8,4096]{1,0:T(8,128)(2,1)S(1)} %collective-permute-done.23), channel_id=1, source_target_pairs={{0,4},{2,6},{4,8},{6,10},{8,12},{10,14},{12,16},{14,18},{16,20},{1... | collective-permute-start | bytes 196616 | tf_op jit(solution)/shard_map/ppermute | solution.py:31
  79.7 1.0 collective-permute-start.26
  80.7 0.7 collective-permute-start.28
  81.4 1.9 %collective-permute-start.29 = (bf16[8,4096]{1,0:T(8,128)(2,1)S(1)}, bf16[8,4096]{1,0:T(8,128)(2,1)S(1)}, u32[]{:S(2)}, u32[]{:S(2)}) collective-permute-start(bf16[8,4096]{1,0:T(8,128)(2,1)S(1)} %collective-permute-done.27), channel_id=1, source_target_pairs={{0,2},{2,4},{4,6},{6,8},{8,10},{10,12},{12,14},{14,16},{16,18},{18... | collective-permute-start | bytes 196616 | tf_op jit(solution)/shard_map/ppermute | solution.py:31
  83.3 2.0 %collective-permute-start.31 = (bf16[8,4096]{1,0:T(8,128)(2,1)S(1)}, bf16[8,4096]{1,0:T(8,128)(2,1)S(1)}, u32[]{:S(2)}, u32[]{:S(2)}) collective-permute-start(bf16[8,4096]{1,0:T(8,128)(2,1)S(1)} %collective-permute-done.27), channel_id=1, source_target_pairs={{0,4},{2,6},{4,8},{6,10},{8,12},{10,14},{12,16},{14,18},{16,20},{1... | collective-permute-start | bytes 196616 | tf_op jit(solution)/shard_map/ppermute | solution.py:31
  92.3 10.7 %collective-permute-start.32 = (bf16[256,4096]{1,0:T(8,128)(2,1)}, bf16[256,4096]{1,0:T(8,128)(2,1)S(1)}, u32[]{:S(2)}, u32[]{:S(2)}) collective-permute-start(bf16[256,4096]{1,0:T(8,128)(2,1)} %get-tuple-element.2), channel_id=1, source_target_pairs={{0,1},{1,0},{2,3},{3,2},{4,5},{5,4},{6,7},{7,6},{8,9},{9,8},{10,11... | collective-permute-start | bytes 6291464 | tf_op jit(solution)/shard_map/ppermute | solution.py:43
  103.0 4.0 %collective-permute-done.32 = bf16[256,4096]{1,0:T(8,128)(2,1)S(1)} collective-permute-done((bf16[256,4096]{1,0:T(8,128)(2,1)}, bf16[256,4096]{1,0:T(8,128)(2,1)S(1)}, u32[]{:S(2)}, u32[]{:S(2)}) %collective-permute-start.32) | collective-permute-done | bytes 2097184 | tf_op jit(solution)/shard_map/ppermute | solution.py:43
  107.0 1.5 %constant_dynamic-update-slice_fusion.32.all_ref = bf16[512,4096]{1,0:T(8,128)(2,1)} fusion(bf16[512,4096]{1,0:T(8,128)(2,1)} %get-tuple-element.3, bf16[256,4096]{1,0:T(8,128)(2,1)S(1)} %collective-permute-done.32), kind=kLoop, calls=%fused_computation.43 | loop fusion | bytes 4194304 | tf_op jit(solution)/shard_map/concatenate | solution.py:43
  108.5 20.7 %fisher_and_solve.1 = (bf16[64,4096]{1,0:T(8,128)(2,1)}, f32[8,4096]{1,0:T(8,128)}) custom-call(s32[1]{0:T(128)} %bitcast.place_ref, bf16[512,4096]{1,0:T(8,128)(2,1)} %constant_dynamic-update-slice_fusion.32.all_ref), custom_call_target="tpu_custom_call" | custom-call | tf_op jit(solution)/shard_map/fisher_and_solve/pallas_call | solution.py:135
  (78 shorter events, 25.1 us)
Async XLA Ops:
  10.4 31.1 %collective-permute-start = (bf16[8,4096]{1,0:T(8,128)(2,1)S(1)}, bf16[8,4096]{1,0:T(8,128)(2,1)S(1)}, u32[]{:S(2)}, u32[]{:S(2)}) collective-permute-start(bf16[8,4096]{1,0:T(8,128)(2,1)S(1)} %convert_element_type.16), channel_id=1, source_target_pairs={{0,2},{2,4},{4,6},{6,8},{8,10},{10,12},{12,14},{14,16},{16,18},{18... | collective-permute-start | bytes 196616 | tf_op jit(solution)/shard_map/ppermute | solution.py:31
  34.1 5.2 %collective-permute-start.3 = (bf16[8,4096]{1,0:T(8,128)(2,1)S(1)}, bf16[8,4096]{1,0:T(8,128)(2,1)S(1)}, u32[]{:S(2)}, u32[]{:S(2)}) collective-permute-start(bf16[8,4096]{1,0:T(8,128)(2,1)S(1)} %convert_element_type.16), channel_id=1, source_target_pairs={{0,4},{2,6},{4,8},{6,10},{8,12},{10,14},{12,16},{14,18},{16,20},{1... | collective-permute-start | bytes 196616 | tf_op jit(solution)/shard_map/ppermute | solution.py:31
  36.8 10.2 %collective-permute-start.2 = (bf16[8,4096]{1,0:T(8,128)(2,1)S(1)}, bf16[8,4096]{1,0:T(8,128)(2,1)S(1)}, u32[]{:S(2)}, u32[]{:S(2)}) collective-permute-start(bf16[8,4096]{1,0:T(8,128)(2,1)S(1)} %collective-permute-done.1), channel_id=1, source_target_pairs={{0,2},{2,4},{4,6},{6,8},{8,10},{10,12},{12,14},{14,16},{16,18},{18... | collective-permute-start | bytes 196616 | tf_op jit(solution)/shard_map/ppermute | solution.py:31
  37.3 4.8 %collective-permute-start.4 = (bf16[8,4096]{1,0:T(8,128)(2,1)S(1)}, bf16[8,4096]{1,0:T(8,128)(2,1)S(1)}, u32[]{:S(2)}, u32[]{:S(2)}) collective-permute-start(bf16[8,4096]{1,0:T(8,128)(2,1)S(1)} %collective-permute-done.1), channel_id=1, source_target_pairs={{0,4},{2,6},{4,8},{6,10},{8,12},{10,14},{12,16},{14,18},{16,20},{1... | collective-permute-start | bytes 196616 | tf_op jit(solution)/shard_map/ppermute | solution.py:31
  39.3 10.5 %collective-permute-start.5 = (bf16[8,4096]{1,0:T(8,128)(2,1)S(1)}, bf16[8,4096]{1,0:T(8,128)(2,1)S(1)}, u32[]{:S(2)}, u32[]{:S(2)}) collective-permute-start(bf16[8,4096]{1,0:T(8,128)(2,1)S(1)} %collective-permute-done.3), channel_id=1, source_target_pairs={{0,2},{2,4},{4,6},{6,8},{8,10},{10,12},{12,14},{14,16},{16,18},{18... | collective-permute-start | bytes 196616 | tf_op jit(solution)/shard_map/ppermute | solution.py:31
  40.8 4.8 %collective-permute-start.7 = (bf16[8,4096]{1,0:T(8,128)(2,1)S(1)}, bf16[8,4096]{1,0:T(8,128)(2,1)S(1)}, u32[]{:S(2)}, u32[]{:S(2)}) collective-permute-start(bf16[8,4096]{1,0:T(8,128)(2,1)S(1)} %collective-permute-done.3), channel_id=1, source_target_pairs={{0,4},{2,6},{4,8},{6,10},{8,12},{10,14},{12,16},{14,18},{16,20},{1... | collective-permute-start | bytes 196616 | tf_op jit(solution)/shard_map/ppermute | solution.py:31
  42.1 11.7 %collective-permute-start.6 = (bf16[8,4096]{1,0:T(8,128)(2,1)S(1)}, bf16[8,4096]{1,0:T(8,128)(2,1)S(1)}, u32[]{:S(2)}, u32[]{:S(2)}) collective-permute-start(bf16[8,4096]{1,0:T(8,128)(2,1)S(1)} %collective-permute-done.4), channel_id=1, source_target_pairs={{0,2},{2,4},{4,6},{6,8},{8,10},{10,12},{12,14},{14,16},{16,18},{18... | collective-permute-start | bytes 196616 | tf_op jit(solution)/shard_map/ppermute | solution.py:31
  43.1 7.3 %collective-permute-start.8 = (bf16[8,4096]{1,0:T(8,128)(2,1)S(1)}, bf16[8,4096]{1,0:T(8,128)(2,1)S(1)}, u32[]{:S(2)}, u32[]{:S(2)}) collective-permute-start(bf16[8,4096]{1,0:T(8,128)(2,1)S(1)} %collective-permute-done.4), channel_id=1, source_target_pairs={{0,4},{2,6},{4,8},{6,10},{8,12},{10,14},{12,16},{14,18},{16,20},{1... | collective-permute-start | bytes 196616 | tf_op jit(solution)/shard_map/ppermute | solution.py:31
  45.5 11.8 %collective-permute-start.9 = (bf16[8,4096]{1,0:T(8,128)(2,1)S(1)}, bf16[8,4096]{1,0:T(8,128)(2,1)S(1)}, u32[]{:S(2)}, u32[]{:S(2)}) collective-permute-start(bf16[8,4096]{1,0:T(8,128)(2,1)S(1)} %collective-permute-done.7), channel_id=1, source_target_pairs={{0,2},{2,4},{4,6},{6,8},{8,10},{10,12},{12,14},{14,16},{16,18},{18... | collective-permute-start | bytes 196616 | tf_op jit(solution)/shard_map/ppermute | solution.py:31
  47.0 6.6 %collective-permute-start.11 = (bf16[8,4096]{1,0:T(8,128)(2,1)S(1)}, bf16[8,4096]{1,0:T(8,128)(2,1)S(1)}, u32[]{:S(2)}, u32[]{:S(2)}) collective-permute-start(bf16[8,4096]{1,0:T(8,128)(2,1)S(1)} %collective-permute-done.7), channel_id=1, source_target_pairs={{0,4},{2,6},{4,8},{6,10},{8,12},{10,14},{12,16},{14,18},{16,20},{1... | collective-permute-start | bytes 196616 | tf_op jit(solution)/shard_map/ppermute | solution.py:31
  50.4 10.6 %collective-permute-start.10 = (bf16[8,4096]{1,0:T(8,128)(2,1)S(1)}, bf16[8,4096]{1,0:T(8,128)(2,1)S(1)}, u32[]{:S(2)}, u32[]{:S(2)}) collective-permute-start(bf16[8,4096]{1,0:T(8,128)(2,1)S(1)} %collective-permute-done.8), channel_id=1, source_target_pairs={{0,2},{2,4},{4,6},{6,8},{8,10},{10,12},{12,14},{14,16},{16,18},{18... | collective-permute-start | bytes 196616 | tf_op jit(solution)/shard_map/ppermute | solution.py:31
  51.9 6.1 %collective-permute-start.12 = (bf16[8,4096]{1,0:T(8,128)(2,1)S(1)}, bf16[8,4096]{1,0:T(8,128)(2,1)S(1)}, u32[]{:S(2)}, u32[]{:S(2)}) collective-permute-start(bf16[8,4096]{1,0:T(8,128)(2,1)S(1)} %collective-permute-done.8), channel_id=1, source_target_pairs={{0,4},{2,6},{4,8},{6,10},{8,12},{10,14},{12,16},{14,18},{16,20},{1... | collective-permute-start | bytes 196616 | tf_op jit(solution)/shard_map/ppermute | solution.py:31
  53.7 10.9 %collective-permute-start.13 = (bf16[8,4096]{1,0:T(8,128)(2,1)S(1)}, bf16[8,4096]{1,0:T(8,128)(2,1)S(1)}, u32[]{:S(2)}, u32[]{:S(2)}) collective-permute-start(bf16[8,4096]{1,0:T(8,128)(2,1)S(1)} %collective-permute-done.11), channel_id=1, source_target_pairs={{0,2},{2,4},{4,6},{6,8},{8,10},{10,12},{12,14},{14,16},{16,18},{18... | collective-permute-start | bytes 196616 | tf_op jit(solution)/shard_map/ppermute | solution.py:31
  53.8 6.4 %collective-permute-start.15 = (bf16[8,4096]{1,0:T(8,128)(2,1)S(1)}, bf16[8,4096]{1,0:T(8,128)(2,1)S(1)}, u32[]{:S(2)}, u32[]{:S(2)}) collective-permute-start(bf16[8,4096]{1,0:T(8,128)(2,1)S(1)} %collective-permute-done.11), channel_id=1, source_target_pairs={{0,4},{2,6},{4,8},{6,10},{8,12},{10,14},{12,16},{14,18},{16,20},{1... | collective-permute-start | bytes 196616 | tf_op jit(solution)/shard_map/ppermute | solution.py:31
  58.0 10.2 %collective-permute-start.14 = (bf16[8,4096]{1,0:T(8,128)(2,1)S(1)}, bf16[8,4096]{1,0:T(8,128)(2,1)S(1)}, u32[]{:S(2)}, u32[]{:S(2)}) collective-permute-start(bf16[8,4096]{1,0:T(8,128)(2,1)S(1)} %collective-permute-done.12), channel_id=1, source_target_pairs={{0,2},{2,4},{4,6},{6,8},{8,10},{10,12},{12,14},{14,16},{16,18},{18... | collective-permute-start | bytes 196616 | tf_op jit(solution)/shard_map/ppermute | solution.py:31
  59.3 5.9 %collective-permute-start.16 = (bf16[8,4096]{1,0:T(8,128)(2,1)S(1)}, bf16[8,4096]{1,0:T(8,128)(2,1)S(1)}, u32[]{:S(2)}, u32[]{:S(2)}) collective-permute-start(bf16[8,4096]{1,0:T(8,128)(2,1)S(1)} %collective-permute-done.12), channel_id=1, source_target_pairs={{0,4},{2,6},{4,8},{6,10},{8,12},{10,14},{12,16},{14,18},{16,20},{1... | collective-permute-start | bytes 196616 | tf_op jit(solution)/shard_map/ppermute | solution.py:31
  60.2 11.2 %collective-permute-start.17 = (bf16[8,4096]{1,0:T(8,128)(2,1)S(1)}, bf16[8,4096]{1,0:T(8,128)(2,1)S(1)}, u32[]{:S(2)}, u32[]{:S(2)}) collective-permute-start(bf16[8,4096]{1,0:T(8,128)(2,1)S(1)} %collective-permute-done.15), channel_id=1, source_target_pairs={{0,2},{2,4},{4,6},{6,8},{8,10},{10,12},{12,14},{14,16},{16,18},{18... | collective-permute-start | bytes 196616 | tf_op jit(solution)/shard_map/ppermute | solution.py:31
  61.0 6.7 %collective-permute-start.19 = (bf16[8,4096]{1,0:T(8,128)(2,1)S(1)}, bf16[8,4096]{1,0:T(8,128)(2,1)S(1)}, u32[]{:S(2)}, u32[]{:S(2)}) collective-permute-start(bf16[8,4096]{1,0:T(8,128)(2,1)S(1)} %collective-permute-done.15), channel_id=1, source_target_pairs={{0,4},{2,6},{4,8},{6,10},{8,12},{10,14},{12,16},{14,18},{16,20},{1... | collective-permute-start | bytes 196616 | tf_op jit(solution)/shard_map/ppermute | solution.py:31
  65.2 9.9 %collective-permute-start.18 = (bf16[8,4096]{1,0:T(8,128)(2,1)S(1)}, bf16[8,4096]{1,0:T(8,128)(2,1)S(1)}, u32[]{:S(2)}, u32[]{:S(2)}) collective-permute-start(bf16[8,4096]{1,0:T(8,128)(2,1)S(1)} %collective-permute-done.16), channel_id=1, source_target_pairs={{0,2},{2,4},{4,6},{6,8},{8,10},{10,12},{12,14},{14,16},{16,18},{18... | collective-permute-start | bytes 196616 | tf_op jit(solution)/shard_map/ppermute | solution.py:31
  65.9 6.2 %collective-permute-start.20 = (bf16[8,4096]{1,0:T(8,128)(2,1)S(1)}, bf16[8,4096]{1,0:T(8,128)(2,1)S(1)}, u32[]{:S(2)}, u32[]{:S(2)}) collective-permute-start(bf16[8,4096]{1,0:T(8,128)(2,1)S(1)} %collective-permute-done.16), channel_id=1, source_target_pairs={{0,4},{2,6},{4,8},{6,10},{8,12},{10,14},{12,16},{14,18},{16,20},{1... | collective-permute-start | bytes 196616 | tf_op jit(solution)/shard_map/ppermute | solution.py:31
  67.8 11.2 %collective-permute-start.21 = (bf16[8,4096]{1,0:T(8,128)(2,1)S(1)}, bf16[8,4096]{1,0:T(8,128)(2,1)S(1)}, u32[]{:S(2)}, u32[]{:S(2)}) collective-permute-start(bf16[8,4096]{1,0:T(8,128)(2,1)S(1)} %collective-permute-done.19), channel_id=1, source_target_pairs={{0,2},{2,4},{4,6},{6,8},{8,10},{10,12},{12,14},{14,16},{16,18},{18... | collective-permute-start | bytes 196616 | tf_op jit(solution)/shard_map/ppermute | solution.py:31
  68.2 5.5 %collective-permute-start.23 = (bf16[8,4096]{1,0:T(8,128)(2,1)S(1)}, bf16[8,4096]{1,0:T(8,128)(2,1)S(1)}, u32[]{:S(2)}, u32[]{:S(2)}) collective-permute-start(bf16[8,4096]{1,0:T(8,128)(2,1)S(1)} %collective-permute-done.19), channel_id=1, source_target_pairs={{0,4},{2,6},{4,8},{6,10},{8,12},{10,14},{12,16},{14,18},{16,20},{1... | collective-permute-start | bytes 196616 | tf_op jit(solution)/shard_map/ppermute | solution.py:31
  72.1 11.3 %collective-permute-start.22 = (bf16[8,4096]{1,0:T(8,128)(2,1)S(1)}, bf16[8,4096]{1,0:T(8,128)(2,1)S(1)}, u32[]{:S(2)}, u32[]{:S(2)}) collective-permute-start(bf16[8,4096]{1,0:T(8,128)(2,1)S(1)} %collective-permute-done.20), channel_id=1, source_target_pairs={{0,2},{2,4},{4,6},{6,8},{8,10},{10,12},{12,14},{14,16},{16,18},{18... | collective-permute-start | bytes 196616 | tf_op jit(solution)/shard_map/ppermute | solution.py:31
  72.5 7.1 %collective-permute-start.24 = (bf16[8,4096]{1,0:T(8,128)(2,1)S(1)}, bf16[8,4096]{1,0:T(8,128)(2,1)S(1)}, u32[]{:S(2)}, u32[]{:S(2)}) collective-permute-start(bf16[8,4096]{1,0:T(8,128)(2,1)S(1)} %collective-permute-done.20), channel_id=1, source_target_pairs={{0,4},{2,6},{4,8},{6,10},{8,12},{10,14},{12,16},{14,18},{16,20},{1... | collective-permute-start | bytes 196616 | tf_op jit(solution)/shard_map/ppermute | solution.py:31
  73.7 13.5 %collective-permute-start.25 = (bf16[8,4096]{1,0:T(8,128)(2,1)S(1)}, bf16[8,4096]{1,0:T(8,128)(2,1)S(1)}, u32[]{:S(2)}, u32[]{:S(2)}) collective-permute-start(bf16[8,4096]{1,0:T(8,128)(2,1)S(1)} %collective-permute-done.23), channel_id=1, source_target_pairs={{0,2},{2,4},{4,6},{6,8},{8,10},{10,12},{12,14},{14,16},{16,18},{18... | collective-permute-start | bytes 196616 | tf_op jit(solution)/shard_map/ppermute | solution.py:31
  75.1 6.2 %collective-permute-start.27 = (bf16[8,4096]{1,0:T(8,128)(2,1)S(1)}, bf16[8,4096]{1,0:T(8,128)(2,1)S(1)}, u32[]{:S(2)}, u32[]{:S(2)}) collective-permute-start(bf16[8,4096]{1,0:T(8,128)(2,1)S(1)} %collective-permute-done.23), channel_id=1, source_target_pairs={{0,4},{2,6},{4,8},{6,10},{8,12},{10,14},{12,16},{14,18},{16,20},{1... | collective-permute-start | bytes 196616 | tf_op jit(solution)/shard_map/ppermute | solution.py:31
  79.7 8.4 %collective-permute-start.26 = (bf16[8,4096]{1,0:T(8,128)(2,1)S(1)}, bf16[8,4096]{1,0:T(8,128)(2,1)S(1)}, u32[]{:S(2)}, u32[]{:S(2)}) collective-permute-start(bf16[8,4096]{1,0:T(8,128)(2,1)S(1)} %collective-permute-done.24), channel_id=1, source_target_pairs={{0,2},{2,4},{4,6},{6,8},{8,10},{10,12},{12,14},{14,16},{16,18},{18... | collective-permute-start | bytes 196616 | tf_op jit(solution)/shard_map/ppermute | solution.py:31
  80.7 7.2 %collective-permute-start.28 = (bf16[8,4096]{1,0:T(8,128)(2,1)S(1)}, bf16[8,4096]{1,0:T(8,128)(2,1)S(1)}, u32[]{:S(2)}, u32[]{:S(2)}) collective-permute-start(bf16[8,4096]{1,0:T(8,128)(2,1)S(1)} %collective-permute-done.24), channel_id=1, source_target_pairs={{0,4},{2,6},{4,8},{6,10},{8,12},{10,14},{12,16},{14,18},{16,20},{1... | collective-permute-start | bytes 196616 | tf_op jit(solution)/shard_map/ppermute | solution.py:31
  81.4 8.6 %collective-permute-start.29 = (bf16[8,4096]{1,0:T(8,128)(2,1)S(1)}, bf16[8,4096]{1,0:T(8,128)(2,1)S(1)}, u32[]{:S(2)}, u32[]{:S(2)}) collective-permute-start(bf16[8,4096]{1,0:T(8,128)(2,1)S(1)} %collective-permute-done.27), channel_id=1, source_target_pairs={{0,2},{2,4},{4,6},{6,8},{8,10},{10,12},{12,14},{14,16},{16,18},{18... | collective-permute-start | bytes 196616 | tf_op jit(solution)/shard_map/ppermute | solution.py:31
  83.3 8.4 %collective-permute-start.31 = (bf16[8,4096]{1,0:T(8,128)(2,1)S(1)}, bf16[8,4096]{1,0:T(8,128)(2,1)S(1)}, u32[]{:S(2)}, u32[]{:S(2)}) collective-permute-start(bf16[8,4096]{1,0:T(8,128)(2,1)S(1)} %collective-permute-done.27), channel_id=1, source_target_pairs={{0,4},{2,6},{4,8},{6,10},{8,12},{10,14},{12,16},{14,18},{16,20},{1... | collective-permute-start | bytes 196616 | tf_op jit(solution)/shard_map/ppermute | solution.py:31
  87.9 3.1 %collective-permute-start.30 = (bf16[8,4096]{1,0:T(8,128)(2,1)S(1)}, bf16[8,4096]{1,0:T(8,128)(2,1)S(1)}, u32[]{:S(2)}, u32[]{:S(2)}) collective-permute-start(bf16[8,4096]{1,0:T(8,128)(2,1)S(1)} %collective-permute-done.28), channel_id=1, source_target_pairs={{0,2},{2,4},{4,6},{6,8},{8,10},{10,12},{12,14},{14,16},{16,18},{18... | collective-permute-start | bytes 196616 | tf_op jit(solution)/shard_map/ppermute | solution.py:31
  92.3 14.7 %collective-permute-start.32 = (bf16[256,4096]{1,0:T(8,128)(2,1)}, bf16[256,4096]{1,0:T(8,128)(2,1)S(1)}, u32[]{:S(2)}, u32[]{:S(2)}) collective-permute-start(bf16[256,4096]{1,0:T(8,128)(2,1)} %get-tuple-element.2), channel_id=1, source_target_pairs={{0,1},{1,0},{2,3},{3,2},{4,5},{5,4},{6,7},{7,6},{8,9},{9,8},{10,11... | collective-permute-start | bytes 6291464 | tf_op jit(solution)/shard_map/ppermute | solution.py:43
  (2 other events, 7.2 us)

commit v2 on v1

--- a/solution.py
+++ b/solution.py
@@ -9,6 +9,7 @@
 
 RESERVED = 32064
 TOLERANCE = 1e-5
+KERNEL_VMEM = 24 * 2**20
 
 
 def project(values, sign_bits):
@@ -39,8 +40,10 @@
         held += [along(value, 1) for value in carried]
         held += onward
         carried = onward
-    half = jnp.concatenate(held, axis=0)
-    return jnp.concatenate([half, lax.ppermute(half, axis, turn)], axis=0)
+    cuts = (0, chips // 2, 3 * chips // 4, chips)
+    halves = [jnp.concatenate(held[low:high], axis=0) for low, high in zip(cuts, cuts[1:])]
+    blocks = [block for half in halves for block in (half, lax.ppermute(half, axis, turn))]
+    return blocks[:-2], blocks[-2:]
 
 
 def split3(value):
@@ -62,11 +65,51 @@
     )
 
 
-def tail_kernel(place_ref, all_ref, fisher_ref, precond_ref, columns_ref, high_ref, mid_ref, low_ref):
-    samples, features = all_ref.shape
+def join(blocks, out_ref):
+    start = 0
+    for block in blocks:
+        out_ref[start : start + block.shape[0]] = block[...]
+        start += block.shape[0]
+
+
+def early_kernel(*refs):
+    *blocks, rows_ref, gram_ref = refs
+    join(blocks, rows_ref)
+    gram_ref[...] = dot(rows_ref[...], rows_ref[...], (1, 1))
+
+
+def early(blocks):
+    count, features = sum(block.shape[0] for block in blocks), blocks[0].shape[1]
+    vmem = pl.BlockSpec(memory_space=pltpu.VMEM)
+    return pl.pallas_call(
+        early_kernel,
+        name="early_gram",
+        out_shape=(
+            jax.ShapeDtypeStruct((count, features), jnp.bfloat16),
+            jax.ShapeDtypeStruct((count, count), jnp.float32),
+        ),
+        in_specs=[vmem] * len(blocks),
+        out_specs=(vmem, vmem),
+        cost_estimate=pl.CostEstimate(
+            flops=2 * count * count * features, bytes_accessed=4 * count * features, transcendentals=0
+        ),
+        compiler_params=pltpu.CompilerParams(vmem_limit_bytes=KERNEL_VMEM),
+    )(*blocks)
+
+
+def tail_kernel(place_ref, first_ref, first_gram_ref, *refs):
+    *blocks, fisher_ref, precond_ref, columns_ref, high_ref, mid_ref, low_ref, late_ref, gram_ref = refs
+    earlier, features = first_ref.shape
+    samples = gram_ref.shape[0]
     own_rows = fisher_ref.shape[0]
     count = precond_ref.shape[0]
-    gram = dot(all_ref[...], all_ref[...], (1, 1))
+    join(blocks, late_ref)
+    late_gram = dot(late_ref[...], first_ref[...], (1, 1))
+    gram_ref[:earlier, :earlier] = first_gram_ref[...]
+    gram_ref[earlier:, :earlier] = late_gram
+    gram_ref[:earlier, earlier:] = late_gram.T
+    gram_ref[earlier:, earlier:] = dot(late_ref[...], late_ref[...], (1, 1))
+    gram = gram_ref[...]
     row = lax.broadcasted_iota(jnp.int32, gram.shape, 0)
     column = lax.broadcasted_iota(jnp.int32, gram.shape, 1)
     on_diagonal = row == column
@@ -120,17 +163,20 @@
     place = place_ref[0]
     lanes = columns_ref.shape[0]
     block = pl.multiple_of((place * own_rows // lanes) * lanes, lanes)
-    columns_ref[...] = all_ref[:, pl.ds(block, lanes)].astype(jnp.float32).T
+    columns_ref[:, :earlier] = first_ref[:, pl.ds(block, lanes)].astype(jnp.float32).T
+    columns_ref[:, earlier:] = late_ref[:, pl.ds(block, lanes)].astype(jnp.float32).T
     inside = pl.multiple_of(place * own_rows % lanes, own_rows)
     columns = columns_ref[pl.ds(inside, own_rows), :].astype(jnp.bfloat16)
-    both = dot(jnp.concatenate([columns, stack3(solved * across)], axis=0), all_ref[...])
+    left = jnp.concatenate([columns, stack3(solved * across)], axis=0)
+    both = dot(left[:, :earlier], first_ref[...]) + dot(left[:, earlier:], late_ref[...])
     fisher_ref[...] = (both[:own_rows] * (1.0 / samples)).astype(jnp.bfloat16)
     low, mid, high = (both[own_rows + k * count : own_rows + (k + 1) * count] for k in (2, 1, 0))
     precond_ref[...] = high + (mid + low)
 
 
-def tail(gathered, place, count, own_rows):
-    samples, features = gathered.shape
+def tail(place, rows, gram, blocks, count, own_rows):
+    late, features = sum(block.shape[0] for block in blocks), rows.shape[1]
+    samples = rows.shape[0] + late
     vmem = pl.BlockSpec(memory_space=pltpu.VMEM)
     return pl.pallas_call(
         tail_kernel,
@@ -139,13 +185,16 @@
             jax.ShapeDtypeStruct((own_rows, features), jnp.bfloat16),
             jax.ShapeDtypeStruct((count, features), jnp.float32),
         ),
-        in_specs=[pl.BlockSpec(memory_space=pltpu.SMEM), vmem],
+        in_specs=[pl.BlockSpec(memory_space=pltpu.SMEM)] + [vmem] * (2 + len(blocks)),
         out_specs=(vmem, vmem),
         scratch_shapes=[
             pltpu.VMEM((128, samples), jnp.float32),
             *[pltpu.VMEM((samples, samples), jnp.bfloat16)] * 3,
+            pltpu.VMEM((late, features), jnp.bfloat16),
+            pltpu.VMEM((samples, samples), jnp.float32),
         ],
-    )(place, gathered)
+        compiler_params=pltpu.CompilerParams(vmem_limit_bytes=KERNEL_VMEM),
+    )(place, rows, gram, *blocks)
 
 
 def on_device(inputs, out_grads, token_ids, in_signs, out_signs):
@@ -155,10 +204,11 @@
     out_proj = project(out_grads, out_signs).reshape(local_count, length, -1)
     outer = jnp.einsum("sti,stj->sij", in_proj, out_proj, precision=lax.Precision.HIGHEST)
     per_sample = outer.reshape(local_count, -1).astype(jnp.bfloat16)
-    gathered = gather_samples(per_sample, "dp")
+    first, last = gather_samples(per_sample, "dp")
+    rows, gram = early(first)
     own_rows = per_sample.shape[1] // lax.axis_size("dp")
     place = lax.axis_index("dp").astype(jnp.int32).reshape(1)
-    return tail(gathered, place, local_count, own_rows)
+    return tail(place, rows, gram, last, local_count, own_rows)
 
 
 def solution(mesh):

time: 129 us -> 116 us (0.90); the launches traced: 129 us -> 114 us
  local copies, waits for them, and re-layouts: 22.7 us -> 0.64 us
  starting transfers between devices: 70.9 us -> 80.3 us
  Pallas kernels: 20.7 us -> 18.2 us
    unnamed x33 -> x31, local copies, waits for them, and re-layouts: 20.1 us -> 0.18 us
    ppermute x31, starting transfers between devices: 60.2 us -> 68.4 us  [along(): return lax.ppermute(value, axis, pairs)]
    pallas_call x1, Pallas kernels: 20.7 us -> 15.1 us  [tail(): pl.pallas_call(tail_kernel, name='fisher_and_solve', out_shape=(jax.Shape...]
    ppermute x31, waiting for transfers between devices: 0.9 us -> 4.93 us  [along(): return lax.ppermute(value, axis, pairs)]
    ppermute x1 -> x3, waiting for transfers between devices: 4 us -> 0.01 us  [gather_samples(): lax.ppermute(half, axis, turn)]
    pallas_call x0 -> x1, Pallas kernels: none -> 3.05 us  [early(): pl.pallas_call(early_kernel, name='early_gram', out_shape=(jax.ShapeDtype...]
    concatenate x2 -> x3, local copies, waits for them, and re-layouts: 2.14 us -> 0.02 us  [gather_samples(): jnp.concatenate(held[low:high], axis=0)]
    ppermute x1 -> x3, starting transfers between devices: 10.7 us -> 11.8 us  [gather_samples(): lax.ppermute(half, axis, turn)]
  transfers between devices with their start and end apart: 33 -> 35, of which waited for: 3 -> 6; matrix products, arithmetic and copies ran while one was open for 16% -> 0% of each run, Pallas kernels for 0% -> 3%
where the time goes in v2:
time: 116 us; the launch traced here: 114 us
  starting transfers between devices  80.3 us (69%)
  Pallas kernels  18.2 us (16%)
  matrix products  8.58 us (7%)
  waiting for transfers between devices  4.94 us (4%)
    ppermute x31, starting transfers between devices, along(): return lax.ppermute(value, axis, pairs)  68.4 us
    pallas_call x1, Pallas kernels, tail(): pl.pallas_call(tail_kernel, name='fisher_and_solve', out_shape=(jax.Shape...  15.1 us
    ppermute x3, starting transfers between devices, gather_samples(): lax.ppermute(half, axis, turn)  11.8 us
    dot_general x2, matrix products, project(): lax.dot_general(flat_rows, sign_table, (((1,), (1,)), ((), ())), preferre...  7.95 us
    ppermute x31, waiting for transfers between devices, along(): return lax.ppermute(value, axis, pairs)  4.93 us
    pallas_call x1, Pallas kernels, early(): pl.pallas_call(early_kernel, name='early_gram', out_shape=(jax.ShapeDtype...  3.05 us
  transfers between devices with their start and end apart: 35, of which 6 were waited for; matrix products, arithmetic and copies ran while one was open for 0% of the time, Pallas kernels for 3%

profile of v2, /device:TPU:37, one launch (start us, length us, event | category | flops | bytes accessed | tf_op | source)
XLA Modules:
  0.0 114.3 jit_solution(9352040539299599930)
XLA Ops:
  1.4 4.4 %fusion.1 = f32[256,64]{0,1:T(8,128)S(1)} fusion(bf16[256,8192]{1,0:T(8,128)(2,1)} %bitcast.14, s32[64,8192]{1,0:T(8,128)} %param.8, f32[256]{0:T(256)S(1)} %mul.33), kind=kOutput, calls=%fused_computation.6 | convolution fusion | flops 270024704 | bytes 6358016 | tf_op jit(solution)/shard_map/dot_general | solution.py:19
  5.9 3.6 %fusion = f32[256,64]{0,1:T(8,128)S(1)} fusion(bf16[256,8192]{1,0:T(8,128)(2,1)} %bitcast.13, s32[64,8192]{1,0:T(8,128)S(1)} %copy-done), kind=kOutput, calls=%fused_computation.4 | convolution fusion | flops 270024704 | bytes 6356992 | tf_op jit(solution)/shard_map/dot_general | solution.py:19
  10.4 23.7 %collective-permute-start = (bf16[8,4096]{1,0:T(8,128)(2,1)S(1)}, bf16[8,4096]{1,0:T(8,128)(2,1)S(1)}, u32[]{:S(2)}, u32[]{:S(2)}) collective-permute-start(bf16[8,4096]{1,0:T(8,128)(2,1)S(1)} %convert_element_type.16), channel_id=1, source_target_pairs={{0,2},{2,4},{4,6},{6,8},{8,10},{10,12},{12,14},{14,16},{16,18},{18... | collective-permute-start | bytes 196616 | tf_op jit(solution)/shard_map/ppermute | solution.py:32
  34.1 2.1 %collective-permute-start.3 = (bf16[8,4096]{1,0:T(8,128)(2,1)S(1)}, bf16[8,4096]{1,0:T(8,128)(2,1)S(1)}, u32[]{:S(2)}, u32[]{:S(2)}) collective-permute-start(bf16[8,4096]{1,0:T(8,128)(2,1)S(1)} %convert_element_type.16), channel_id=1, source_target_pairs={{0,4},{2,6},{4,8},{6,10},{8,12},{10,14},{12,16},{14,18},{16,20},{1... | collective-permute-start | bytes 196616 | tf_op jit(solution)/shard_map/ppermute | solution.py:32
  36.8 2.0 %collective-permute-start.4 = (bf16[8,4096]{1,0:T(8,128)(2,1)S(1)}, bf16[8,4096]{1,0:T(8,128)(2,1)S(1)}, u32[]{:S(2)}, u32[]{:S(2)}) collective-permute-start(bf16[8,4096]{1,0:T(8,128)(2,1)S(1)} %collective-permute-done.1), channel_id=1, source_target_pairs={{0,4},{2,6},{4,8},{6,10},{8,12},{10,14},{12,16},{14,18},{16,20},{1... | collective-permute-start | bytes 196616 | tf_op jit(solution)/shard_map/ppermute | solution.py:32
  38.8 2.0 %collective-permute-start.5 = (bf16[8,4096]{1,0:T(8,128)(2,1)S(1)}, bf16[8,4096]{1,0:T(8,128)(2,1)S(1)}, u32[]{:S(2)}, u32[]{:S(2)}) collective-permute-start(bf16[8,4096]{1,0:T(8,128)(2,1)S(1)} %collective-permute-done.3), channel_id=1, source_target_pairs={{0,2},{2,4},{4,6},{6,8},{8,10},{10,12},{12,14},{14,16},{16,18},{18... | collective-permute-start | bytes 196616 | tf_op jit(solution)/shard_map/ppermute | solution.py:32
  41.5 1.1 collective-permute-start.6
  42.6 2.0 %collective-permute-start.8 = (bf16[8,4096]{1,0:T(8,128)(2,1)S(1)}, bf16[8,4096]{1,0:T(8,128)(2,1)S(1)}, u32[]{:S(2)}, u32[]{:S(2)}) collective-permute-start(bf16[8,4096]{1,0:T(8,128)(2,1)S(1)} %collective-permute-done.4), channel_id=1, source_target_pairs={{0,4},{2,6},{4,8},{6,10},{8,12},{10,14},{12,16},{14,18},{16,20},{1... | collective-permute-start | bytes 196616 | tf_op jit(solution)/shard_map/ppermute | solution.py:32
  44.9 2.8 %collective-permute-start.9 = (bf16[8,4096]{1,0:T(8,128)(2,1)S(1)}, bf16[8,4096]{1,0:T(8,128)(2,1)S(1)}, u32[]{:S(2)}, u32[]{:S(2)}) collective-permute-start(bf16[8,4096]{1,0:T(8,128)(2,1)S(1)} %collective-permute-done.7), channel_id=1, source_target_pairs={{0,2},{2,4},{4,6},{6,8},{8,10},{10,12},{12,14},{14,16},{16,18},{18... | collective-permute-start | bytes 196616 | tf_op jit(solution)/shard_map/ppermute | solution.py:32
  47.8 2.3 %collective-permute-start.10 = (bf16[8,4096]{1,0:T(8,128)(2,1)S(1)}, bf16[8,4096]{1,0:T(8,128)(2,1)S(1)}, u32[]{:S(2)}, u32[]{:S(2)}) collective-permute-start(bf16[8,4096]{1,0:T(8,128)(2,1)S(1)} %collective-permute-done.8), channel_id=1, source_target_pairs={{0,2},{2,4},{4,6},{6,8},{8,10},{10,12},{12,14},{14,16},{16,18},{18... | collective-permute-start | bytes 196616 | tf_op jit(solution)/shard_map/ppermute | solution.py:32
  50.0 1.5 %collective-permute-start.12 = (bf16[8,4096]{1,0:T(8,128)(2,1)S(1)}, bf16[8,4096]{1,0:T(8,128)(2,1)S(1)}, u32[]{:S(2)}, u32[]{:S(2)}) collective-permute-start(bf16[8,4096]{1,0:T(8,128)(2,1)S(1)} %collective-permute-done.8), channel_id=1, source_target_pairs={{0,4},{2,6},{4,8},{6,10},{8,12},{10,14},{12,16},{14,18},{16,20},{1... | collective-permute-start | bytes 196616 | tf_op jit(solution)/shard_map/ppermute | solution.py:32
  52.0 1.0 collective-permute-start.13
  53.0 1.4 %collective-permute-start.15 = (bf16[8,4096]{1,0:T(8,128)(2,1)S(1)}, bf16[8,4096]{1,0:T(8,128)(2,1)S(1)}, u32[]{:S(2)}, u32[]{:S(2)}) collective-permute-start(bf16[8,4096]{1,0:T(8,128)(2,1)S(1)} %collective-permute-done.11), channel_id=1, source_target_pairs={{0,4},{2,6},{4,8},{6,10},{8,12},{10,14},{12,16},{14,18},{16,20},{1... | collective-permute-start | bytes 196616 | tf_op jit(solution)/shard_map/ppermute | solution.py:32
  55.6 1.6 %collective-permute-start.17 = (bf16[8,4096]{1,0:T(8,128)(2,1)S(1)}, bf16[8,4096]{1,0:T(8,128)(2,1)S(1)}, u32[]{:S(2)}, u32[]{:S(2)}) collective-permute-start(bf16[8,4096]{1,0:T(8,128)(2,1)S(1)} %collective-permute-done.12), channel_id=1, source_target_pairs={{0,4},{2,6},{4,8},{6,10},{8,12},{10,14},{12,16},{14,18},{16,20},{1... | collective-permute-start | bytes 196616 | tf_op jit(solution)/shard_map/ppermute | solution.py:32
  57.8 2.5 %collective-permute-start.18 = (bf16[8,4096]{1,0:T(8,128)(2,1)S(1)}, bf16[8,4096]{1,0:T(8,128)(2,1)S(1)}, u32[]{:S(2)}, u32[]{:S(2)}) collective-permute-start(bf16[8,4096]{1,0:T(8,128)(2,1)S(1)} %collective-permute-done.15), channel_id=1, source_target_pairs={{0,2},{2,4},{4,6},{6,8},{8,10},{10,12},{12,14},{14,16},{16,18},{18... | collective-permute-start | bytes 196616 | tf_op jit(solution)/shard_map/ppermute | solution.py:32
  60.5 4.4 %collective-permute-start.16 = (bf16[128,4096]{1,0:T(8,128)(2,1)S(1)}, bf16[128,4096]{1,0:T(8,128)(2,1)}, u32[]{:S(2)}, u32[]{:S(2)}) collective-permute-start(bf16[128,4096]{1,0:T(8,128)(2,1)S(1)} %constant_dynamic-update-slice_fusion.refs_0_), channel_id=1, source_target_pairs={{0,1},{1,0},{2,3},{3,2},{4,5},{5,4},{6,7},{7,6},{8,9},{9,8},{10,11... | collective-permute-start | bytes 3145736 | tf_op jit(solution)/shard_map/ppermute | solution.py:45
  64.9 2.5 %collective-permute-start.19 = (bf16[8,4096]{1,0:T(8,128)(2,1)S(1)}, bf16[8,4096]{1,0:T(8,128)(2,1)S(1)}, u32[]{:S(2)}, u32[]{:S(2)}) collective-permute-start(bf16[8,4096]{1,0:T(8,128)(2,1)S(1)} %collective-permute-done.17), channel_id=1, source_target_pairs={{0,2},{2,4},{4,6},{6,8},{8,10},{10,12},{12,14},{14,16},{16,18},{18... | collective-permute-start | bytes 196616 | tf_op jit(solution)/shard_map/ppermute | solution.py:32
  67.4 1.6 %collective-permute-start.21 = (bf16[8,4096]{1,0:T(8,128)(2,1)S(1)}, bf16[8,4096]{1,0:T(8,128)(2,1)S(1)}, u32[]{:S(2)}, u32[]{:S(2)}) collective-permute-start(bf16[8,4096]{1,0:T(8,128)(2,1)S(1)} %collective-permute-done.17), channel_id=1, source_target_pairs={{0,4},{2,6},{4,8},{6,10},{8,12},{10,14},{12,16},{14,18},{16,20},{1... | collective-permute-start | bytes 196616 | tf_op jit(solution)/shard_map/ppermute | solution.py:32
  69.2 0.9 collective-permute-start.24
  70.1 1.6 %collective-permute-done.21 = bf16[8,4096]{1,0:T(8,128)(2,1)S(1)} collective-permute-done((bf16[8,4096]{1,0:T(8,128)(2,1)S(1)}, bf16[8,4096]{1,0:T(8,128)(2,1)S(1)}, u32[]{:S(2)}, u32[]{:S(2)}) %collective-permute-start.21) | collective-permute-done | bytes 65568 | tf_op jit(solution)/shard_map/ppermute | solution.py:32
  71.7 2.9 %collective-permute-start.23 = (bf16[8,4096]{1,0:T(8,128)(2,1)S(1)}, bf16[8,4096]{1,0:T(8,128)(2,1)S(1)}, u32[]{:S(2)}, u32[]{:S(2)}) collective-permute-start(bf16[8,4096]{1,0:T(8,128)(2,1)S(1)} %collective-permute-done.21), channel_id=1, source_target_pairs={{0,2},{2,4},{4,6},{6,8},{8,10},{10,12},{12,14},{14,16},{16,18},{18... | collective-permute-start | bytes 196616 | tf_op jit(solution)/shard_map/ppermute | solution.py:32
  74.7 1.7 %collective-permute-start.27 = (bf16[8,4096]{1,0:T(8,128)(2,1)S(1)}, bf16[8,4096]{1,0:T(8,128)(2,1)S(1)}, u32[]{:S(2)}, u32[]{:S(2)}) collective-permute-start(bf16[8,4096]{1,0:T(8,128)(2,1)S(1)} %collective-permute-done.24), channel_id=1, source_target_pairs={{0,2},{2,4},{4,6},{6,8},{8,10},{10,12},{12,14},{14,16},{16,18},{18... | collective-permute-start | bytes 196616 | tf_op jit(solution)/shard_map/ppermute | solution.py:32
  76.3 1.0 collective-permute-start.29
  77.4 2.6 %collective-permute-start.25 = (bf16[64,4096]{1,0:T(8,128)(2,1)S(1)}, bf16[64,4096]{1,0:T(8,128)(2,1)S(1)}, u32[]{:S(2)}, u32[]{:S(2)}) collective-permute-start(bf16[64,4096]{1,0:T(8,128)(2,1)S(1)} %constant_dynamic-update-slice_fusion.16.refs_2_), channel_id=1, source_target_pairs={{0,1},{1,0},{2,3},{3,2},{4,5},{5,4},{6,7},{7,6},{8,9},{9,8},{10,11... | collective-permute-start | bytes 1572872 | tf_op jit(solution)/shard_map/ppermute | solution.py:45
  80.1 2.5 %collective-permute-start.28 = (bf16[8,4096]{1,0:T(8,128)(2,1)S(1)}, bf16[8,4096]{1,0:T(8,128)(2,1)S(1)}, u32[]{:S(2)}, u32[]{:S(2)}) collective-permute-start(bf16[8,4096]{1,0:T(8,128)(2,1)S(1)} %collective-permute-done.26), channel_id=1, source_target_pairs={{0,2},{2,4},{4,6},{6,8},{8,10},{10,12},{12,14},{14,16},{16,18},{18... | collective-permute-start | bytes 196616 | tf_op jit(solution)/shard_map/ppermute | solution.py:32
  82.6 1.6 %collective-permute-start.30 = (bf16[8,4096]{1,0:T(8,128)(2,1)S(1)}, bf16[8,4096]{1,0:T(8,128)(2,1)S(1)}, u32[]{:S(2)}, u32[]{:S(2)}) collective-permute-start(bf16[8,4096]{1,0:T(8,128)(2,1)S(1)} %collective-permute-done.26), channel_id=1, source_target_pairs={{0,4},{2,6},{4,8},{6,10},{8,12},{10,14},{12,16},{14,18},{16,20},{1... | collective-permute-start | bytes 196616 | tf_op jit(solution)/shard_map/ppermute | solution.py:32
  84.4 3.0 %collective-permute-start.33 = (bf16[8,4096]{1,0:T(8,128)(2,1)S(1)}, bf16[8,4096]{1,0:T(8,128)(2,1)S(1)}, u32[]{:S(2)}, u32[]{:S(2)}) collective-permute-start(bf16[8,4096]{1,0:T(8,128)(2,1)S(1)} %collective-permute-done.29), channel_id=1, source_target_pairs={{0,4},{2,6},{4,8},{6,10},{8,12},{10,14},{12,16},{14,18},{16,20},{1... | collective-permute-start | bytes 196616 | tf_op jit(solution)/shard_map/ppermute | solution.py:32
  87.4 2.4 %collective-permute-start.32 = (bf16[8,4096]{1,0:T(8,128)(2,1)S(1)}, bf16[8,4096]{1,0:T(8,128)(2,1)S(1)}, u32[]{:S(2)}, u32[]{:S(2)}) collective-permute-start(bf16[8,4096]{1,0:T(8,128)(2,1)S(1)} %collective-permute-done.30), channel_id=1, source_target_pairs={{0,2},{2,4},{4,6},{6,8},{8,10},{10,12},{12,14},{14,16},{16,18},{18... | collective-permute-start | bytes 196616 | tf_op jit(solution)/shard_map/ppermute | solution.py:32
  89.9 1.3 %collective-permute-done.32 = bf16[8,4096]{1,0:T(8,128)(2,1)S(1)} collective-permute-done((bf16[8,4096]{1,0:T(8,128)(2,1)S(1)}, bf16[8,4096]{1,0:T(8,128)(2,1)S(1)}, u32[]{:S(2)}, u32[]{:S(2)}) %collective-permute-start.32) | collective-permute-done | bytes 65568 | tf_op jit(solution)/shard_map/ppermute | solution.py:32
  91.2 4.8 %collective-permute-start.34 = (bf16[64,4096]{1,0:T(8,128)(2,1)S(1)}, bf16[64,4096]{1,0:T(8,128)(2,1)S(1)}, u32[]{:S(2)}, u32[]{:S(2)}) collective-permute-start(bf16[64,4096]{1,0:T(8,128)(2,1)S(1)} %constant_dynamic-update-slice_fusion.24.refs_0_), channel_id=1, source_target_pairs={{0,1},{1,0},{2,3},{3,2},{4,5},{5,4},{6,7},{7,6},{8,9},{9,8},{10,11... | collective-permute-start | bytes 1572872 | tf_op jit(solution)/shard_map/ppermute | solution.py:45
  96.0 3.1 %early_gram.1 = (bf16[384,4096]{1,0:T(8,128)(2,1)S(1)}, f32[384,384]{1,0:T(8,128)S(1)}) custom-call(bf16[128,4096]{1,0:T(8,128)(2,1)S(1)} %constant_dynamic-update-slice_fusion.refs_0_, bf16[128,4096]{1,0:T(8,128)(2,1)} %collective-permute-done.16.refs_1_, bf16[64,4096]{1,0:T(8,128)(2,1)S(1)} %constant_dynamic-update-slice_fusion.16.refs_2_, ...), custom_call_target="tpu_custom_call" | custom-call | flops 1207959552 | bytes 6291456 | tf_op jit(solution)/shard_map/early_gram/pallas_call | solution.py:84
  99.1 15.1 %fisher_and_solve.1 = (bf16[64,4096]{1,0:T(8,128)(2,1)}, f32[8,4096]{1,0:T(8,128)}) custom-call(s32[1]{0:T(128)} %bitcast.place_ref, bf16[384,4096]{1,0:T(8,128)(2,1)S(1)} %get-tuple-element.4.first_ref, f32[384,384]{1,0:T(8,128)S(1)} %get-tuple-element.5.first_gram_ref, bf16[64,4096]{1,0:T(8,128)(2,1)S(1)} %constant_dynamic-update-slice_fusion.24.refs_0_, ...), custom_call_target="tpu_custom_call" | custom-call | tf_op jit(solution)/shard_map/fisher_and_solve/pallas_call | solution.py:181
  (82 shorter events, 6.5 us)
Async XLA Ops:
  10.4 31.1 %collective-permute-start = (bf16[8,4096]{1,0:T(8,128)(2,1)S(1)}, bf16[8,4096]{1,0:T(8,128)(2,1)S(1)}, u32[]{:S(2)}, u32[]{:S(2)}) collective-permute-start(bf16[8,4096]{1,0:T(8,128)(2,1)S(1)} %convert_element_type.16), channel_id=1, source_target_pairs={{0,2},{2,4},{4,6},{6,8},{8,10},{10,12},{12,14},{14,16},{16,18},{18... | collective-permute-start | bytes 196616 | tf_op jit(solution)/shard_map/ppermute | solution.py:32
  34.1 4.7 %collective-permute-start.3 = (bf16[8,4096]{1,0:T(8,128)(2,1)S(1)}, bf16[8,4096]{1,0:T(8,128)(2,1)S(1)}, u32[]{:S(2)}, u32[]{:S(2)}) collective-permute-start(bf16[8,4096]{1,0:T(8,128)(2,1)S(1)} %convert_element_type.16), channel_id=1, source_target_pairs={{0,4},{2,6},{4,8},{6,10},{8,12},{10,14},{12,16},{14,18},{16,20},{1... | collective-permute-start | bytes 196616 | tf_op jit(solution)/shard_map/ppermute | solution.py:32
  36.1 11.5 %collective-permute-start.2 = (bf16[8,4096]{1,0:T(8,128)(2,1)S(1)}, bf16[8,4096]{1,0:T(8,128)(2,1)S(1)}, u32[]{:S(2)}, u32[]{:S(2)}) collective-permute-start(bf16[8,4096]{1,0:T(8,128)(2,1)S(1)} %collective-permute-done.1), channel_id=1, source_target_pairs={{0,2},{2,4},{4,6},{6,8},{8,10},{10,12},{12,14},{14,16},{16,18},{18... | collective-permute-start | bytes 196616 | tf_op jit(solution)/shard_map/ppermute | solution.py:32
  36.8 4.7 %collective-permute-start.4 = (bf16[8,4096]{1,0:T(8,128)(2,1)S(1)}, bf16[8,4096]{1,0:T(8,128)(2,1)S(1)}, u32[]{:S(2)}, u32[]{:S(2)}) collective-permute-start(bf16[8,4096]{1,0:T(8,128)(2,1)S(1)} %collective-permute-done.1), channel_id=1, source_target_pairs={{0,4},{2,6},{4,8},{6,10},{8,12},{10,14},{12,16},{14,18},{16,20},{1... | collective-permute-start | bytes 196616 | tf_op jit(solution)/shard_map/ppermute | solution.py:32
  38.8 9.0 %collective-permute-start.5 = (bf16[8,4096]{1,0:T(8,128)(2,1)S(1)}, bf16[8,4096]{1,0:T(8,128)(2,1)S(1)}, u32[]{:S(2)}, u32[]{:S(2)}) collective-permute-start(bf16[8,4096]{1,0:T(8,128)(2,1)S(1)} %collective-permute-done.3), channel_id=1, source_target_pairs={{0,2},{2,4},{4,6},{6,8},{8,10},{10,12},{12,14},{14,16},{16,18},{18... | collective-permute-start | bytes 196616 | tf_op jit(solution)/shard_map/ppermute | solution.py:32
  41.5 11.5 %collective-permute-start.6 = (bf16[8,4096]{1,0:T(8,128)(2,1)S(1)}, bf16[8,4096]{1,0:T(8,128)(2,1)S(1)}, u32[]{:S(2)}, u32[]{:S(2)}) collective-permute-start(bf16[8,4096]{1,0:T(8,128)(2,1)S(1)} %collective-permute-done.4), channel_id=1, source_target_pairs={{0,2},{2,4},{4,6},{6,8},{8,10},{10,12},{12,14},{14,16},{16,18},{18... | collective-permute-start | bytes 196616 | tf_op jit(solution)/shard_map/ppermute | solution.py:32
  42.6 5.2 %collective-permute-start.8 = (bf16[8,4096]{1,0:T(8,128)(2,1)S(1)}, bf16[8,4096]{1,0:T(8,128)(2,1)S(1)}, u32[]{:S(2)}, u32[]{:S(2)}) collective-permute-start(bf16[8,4096]{1,0:T(8,128)(2,1)S(1)} %collective-permute-done.4), channel_id=1, source_target_pairs={{0,4},{2,6},{4,8},{6,10},{8,12},{10,14},{12,16},{14,18},{16,20},{1... | collective-permute-start | bytes 196616 | tf_op jit(solution)/shard_map/ppermute | solution.py:32
  44.9 9.6 %collective-permute-start.9 = (bf16[8,4096]{1,0:T(8,128)(2,1)S(1)}, bf16[8,4096]{1,0:T(8,128)(2,1)S(1)}, u32[]{:S(2)}, u32[]{:S(2)}) collective-permute-start(bf16[8,4096]{1,0:T(8,128)(2,1)S(1)} %collective-permute-done.7), channel_id=1, source_target_pairs={{0,2},{2,4},{4,6},{6,8},{8,10},{10,12},{12,14},{14,16},{16,18},{18... | collective-permute-start | bytes 196616 | tf_op jit(solution)/shard_map/ppermute | solution.py:32
  47.7 4.3 %collective-permute-start.11 = (bf16[8,4096]{1,0:T(8,128)(2,1)S(1)}, bf16[8,4096]{1,0:T(8,128)(2,1)S(1)}, u32[]{:S(2)}, u32[]{:S(2)}) collective-permute-start(bf16[8,4096]{1,0:T(8,128)(2,1)S(1)} %collective-permute-done.7), channel_id=1, source_target_pairs={{0,4},{2,6},{4,8},{6,10},{8,12},{10,14},{12,16},{14,18},{16,20},{1... | collective-permute-start | bytes 196616 | tf_op jit(solution)/shard_map/ppermute | solution.py:32
  47.8 12.6 %collective-permute-start.10 = (bf16[8,4096]{1,0:T(8,128)(2,1)S(1)}, bf16[8,4096]{1,0:T(8,128)(2,1)S(1)}, u32[]{:S(2)}, u32[]{:S(2)}) collective-permute-start(bf16[8,4096]{1,0:T(8,128)(2,1)S(1)} %collective-permute-done.8), channel_id=1, source_target_pairs={{0,2},{2,4},{4,6},{6,8},{8,10},{10,12},{12,14},{14,16},{16,18},{18... | collective-permute-start | bytes 196616 | tf_op jit(solution)/shard_map/ppermute | solution.py:32
  50.0 4.9 %collective-permute-start.12 = (bf16[8,4096]{1,0:T(8,128)(2,1)S(1)}, bf16[8,4096]{1,0:T(8,128)(2,1)S(1)}, u32[]{:S(2)}, u32[]{:S(2)}) collective-permute-start(bf16[8,4096]{1,0:T(8,128)(2,1)S(1)} %collective-permute-done.8), channel_id=1, source_target_pairs={{0,4},{2,6},{4,8},{6,10},{8,12},{10,14},{12,16},{14,18},{16,20},{1... | collective-permute-start | bytes 196616 | tf_op jit(solution)/shard_map/ppermute | solution.py:32
  52.0 8.4 %collective-permute-start.13 = (bf16[8,4096]{1,0:T(8,128)(2,1)S(1)}, bf16[8,4096]{1,0:T(8,128)(2,1)S(1)}, u32[]{:S(2)}, u32[]{:S(2)}) collective-permute-start(bf16[8,4096]{1,0:T(8,128)(2,1)S(1)} %collective-permute-done.11), channel_id=1, source_target_pairs={{0,2},{2,4},{4,6},{6,8},{8,10},{10,12},{12,14},{14,16},{16,18},{18... | collective-permute-start | bytes 196616 | tf_op jit(solution)/shard_map/ppermute | solution.py:32
  53.0 4.8 %collective-permute-start.15 = (bf16[8,4096]{1,0:T(8,128)(2,1)S(1)}, bf16[8,4096]{1,0:T(8,128)(2,1)S(1)}, u32[]{:S(2)}, u32[]{:S(2)}) collective-permute-start(bf16[8,4096]{1,0:T(8,128)(2,1)S(1)} %collective-permute-done.11), channel_id=1, source_target_pairs={{0,4},{2,6},{4,8},{6,10},{8,12},{10,14},{12,16},{14,18},{16,20},{1... | collective-permute-start | bytes 196616 | tf_op jit(solution)/shard_map/ppermute | solution.py:32
  54.9 5.5 %collective-permute-start.14 = (bf16[8,4096]{1,0:T(8,128)(2,1)S(1)}, bf16[8,4096]{1,0:T(8,128)(2,1)S(1)}, u32[]{:S(2)}, u32[]{:S(2)}) collective-permute-start(bf16[8,4096]{1,0:T(8,128)(2,1)S(1)} %collective-permute-done.12), channel_id=1, source_target_pairs={{0,2},{2,4},{4,6},{6,8},{8,10},{10,12},{12,14},{14,16},{16,18},{18... | collective-permute-start | bytes 196616 | tf_op jit(solution)/shard_map/ppermute | solution.py:32
  55.6 9.2 %collective-permute-start.17 = (bf16[8,4096]{1,0:T(8,128)(2,1)S(1)}, bf16[8,4096]{1,0:T(8,128)(2,1)S(1)}, u32[]{:S(2)}, u32[]{:S(2)}) collective-permute-start(bf16[8,4096]{1,0:T(8,128)(2,1)S(1)} %collective-permute-done.12), channel_id=1, source_target_pairs={{0,4},{2,6},{4,8},{6,10},{8,12},{10,14},{12,16},{14,18},{16,20},{1... | collective-permute-start | bytes 196616 | tf_op jit(solution)/shard_map/ppermute | solution.py:32
  57.8 11.3 %collective-permute-start.18 = (bf16[8,4096]{1,0:T(8,128)(2,1)S(1)}, bf16[8,4096]{1,0:T(8,128)(2,1)S(1)}, u32[]{:S(2)}, u32[]{:S(2)}) collective-permute-start(bf16[8,4096]{1,0:T(8,128)(2,1)S(1)} %collective-permute-done.15), channel_id=1, source_target_pairs={{0,2},{2,4},{4,6},{6,8},{8,10},{10,12},{12,14},{14,16},{16,18},{18... | collective-permute-start | bytes 196616 | tf_op jit(solution)/shard_map/ppermute | solution.py:32
  60.4 8.6 %collective-permute-start.20 = (bf16[8,4096]{1,0:T(8,128)(2,1)S(1)}, bf16[8,4096]{1,0:T(8,128)(2,1)S(1)}, u32[]{:S(2)}, u32[]{:S(2)}) collective-permute-start(bf16[8,4096]{1,0:T(8,128)(2,1)S(1)} %collective-permute-done.15), channel_id=1, source_target_pairs={{0,4},{2,6},{4,8},{6,10},{8,12},{10,14},{12,16},{14,18},{16,20},{1... | collective-permute-start | bytes 196616 | tf_op jit(solution)/shard_map/ppermute | solution.py:32
  60.5 35.6 %collective-permute-start.16 = (bf16[128,4096]{1,0:T(8,128)(2,1)S(1)}, bf16[128,4096]{1,0:T(8,128)(2,1)}, u32[]{:S(2)}, u32[]{:S(2)}) collective-permute-start(bf16[128,4096]{1,0:T(8,128)(2,1)S(1)} %constant_dynamic-update-slice_fusion.refs_0_), channel_id=1, source_target_pairs={{0,1},{1,0},{2,3},{3,2},{4,5},{5,4},{6,7},{7,6},{8,9},{9,8},{10,11... | collective-permute-start | bytes 3145736 | tf_op jit(solution)/shard_map/ppermute | solution.py:45
  64.9 9.7 %collective-permute-start.19 = (bf16[8,4096]{1,0:T(8,128)(2,1)S(1)}, bf16[8,4096]{1,0:T(8,128)(2,1)S(1)}, u32[]{:S(2)}, u32[]{:S(2)}) collective-permute-start(bf16[8,4096]{1,0:T(8,128)(2,1)S(1)} %collective-permute-done.17), channel_id=1, source_target_pairs={{0,2},{2,4},{4,6},{6,8},{8,10},{10,12},{12,14},{14,16},{16,18},{18... | collective-permute-start | bytes 196616 | tf_op jit(solution)/shard_map/ppermute | solution.py:32
  67.4 4.3 %collective-permute-start.21 = (bf16[8,4096]{1,0:T(8,128)(2,1)S(1)}, bf16[8,4096]{1,0:T(8,128)(2,1)S(1)}, u32[]{:S(2)}, u32[]{:S(2)}) collective-permute-start(bf16[8,4096]{1,0:T(8,128)(2,1)S(1)} %collective-permute-done.17), channel_id=1, source_target_pairs={{0,4},{2,6},{4,8},{6,10},{8,12},{10,14},{12,16},{14,18},{16,20},{1... | collective-permute-start | bytes 196616 | tf_op jit(solution)/shard_map/ppermute | solution.py:32
  69.0 7.4 %collective-permute-start.22 = (bf16[8,4096]{1,0:T(8,128)(2,1)S(1)}, bf16[8,4096]{1,0:T(8,128)(2,1)S(1)}, u32[]{:S(2)}, u32[]{:S(2)}) collective-permute-start(bf16[8,4096]{1,0:T(8,128)(2,1)S(1)} %collective-permute-done.20), channel_id=1, source_target_pairs={{0,2},{2,4},{4,6},{6,8},{8,10},{10,12},{12,14},{14,16},{16,18},{18... | collective-permute-start | bytes 196616 | tf_op jit(solution)/shard_map/ppermute | solution.py:32
  69.2 5.5 %collective-permute-start.24 = (bf16[8,4096]{1,0:T(8,128)(2,1)S(1)}, bf16[8,4096]{1,0:T(8,128)(2,1)S(1)}, u32[]{:S(2)}, u32[]{:S(2)}) collective-permute-start(bf16[8,4096]{1,0:T(8,128)(2,1)S(1)} %collective-permute-done.20), channel_id=1, source_target_pairs={{0,4},{2,6},{4,8},{6,10},{8,12},{10,14},{12,16},{14,18},{16,20},{1... | collective-permute-start | bytes 196616 | tf_op jit(solution)/shard_map/ppermute | solution.py:32
  71.7 5.7 %collective-permute-start.23 = (bf16[8,4096]{1,0:T(8,128)(2,1)S(1)}, bf16[8,4096]{1,0:T(8,128)(2,1)S(1)}, u32[]{:S(2)}, u32[]{:S(2)}) collective-permute-start(bf16[8,4096]{1,0:T(8,128)(2,1)S(1)} %collective-permute-done.21), channel_id=1, source_target_pairs={{0,2},{2,4},{4,6},{6,8},{8,10},{10,12},{12,14},{14,16},{16,18},{18... | collective-permute-start | bytes 196616 | tf_op jit(solution)/shard_map/ppermute | solution.py:32
  74.6 5.4 %collective-permute-start.26 = (bf16[8,4096]{1,0:T(8,128)(2,1)S(1)}, bf16[8,4096]{1,0:T(8,128)(2,1)S(1)}, u32[]{:S(2)}, u32[]{:S(2)}) collective-permute-start(bf16[8,4096]{1,0:T(8,128)(2,1)S(1)} %collective-permute-done.21), channel_id=1, source_target_pairs={{0,4},{2,6},{4,8},{6,10},{8,12},{10,14},{12,16},{14,18},{16,20},{1... | collective-permute-start | bytes 196616 | tf_op jit(solution)/shard_map/ppermute | solution.py:32
  74.7 7.9 %collective-permute-start.27 = (bf16[8,4096]{1,0:T(8,128)(2,1)S(1)}, bf16[8,4096]{1,0:T(8,128)(2,1)S(1)}, u32[]{:S(2)}, u32[]{:S(2)}) collective-permute-start(bf16[8,4096]{1,0:T(8,128)(2,1)S(1)} %collective-permute-done.24), channel_id=1, source_target_pairs={{0,2},{2,4},{4,6},{6,8},{8,10},{10,12},{12,14},{14,16},{16,18},{18... | collective-permute-start | bytes 196616 | tf_op jit(solution)/shard_map/ppermute | solution.py:32
  76.3 7.8 %collective-permute-start.29 = (bf16[8,4096]{1,0:T(8,128)(2,1)S(1)}, bf16[8,4096]{1,0:T(8,128)(2,1)S(1)}, u32[]{:S(2)}, u32[]{:S(2)}) collective-permute-start(bf16[8,4096]{1,0:T(8,128)(2,1)S(1)} %collective-permute-done.24), channel_id=1, source_target_pairs={{0,4},{2,6},{4,8},{6,10},{8,12},{10,14},{12,16},{14,18},{16,20},{1... | collective-permute-start | bytes 196616 | tf_op jit(solution)/shard_map/ppermute | solution.py:32
  77.4 18.6 %collective-permute-start.25 = (bf16[64,4096]{1,0:T(8,128)(2,1)S(1)}, bf16[64,4096]{1,0:T(8,128)(2,1)S(1)}, u32[]{:S(2)}, u32[]{:S(2)}) collective-permute-start(bf16[64,4096]{1,0:T(8,128)(2,1)S(1)} %constant_dynamic-update-slice_fusion.16.refs_2_), channel_id=1, source_target_pairs={{0,1},{1,0},{2,3},{3,2},{4,5},{5,4},{6,7},{7,6},{8,9},{9,8},{10,11... | collective-permute-start | bytes 1572872 | tf_op jit(solution)/shard_map/ppermute | solution.py:45
  80.1 4.4 %collective-permute-start.28 = (bf16[8,4096]{1,0:T(8,128)(2,1)S(1)}, bf16[8,4096]{1,0:T(8,128)(2,1)S(1)}, u32[]{:S(2)}, u32[]{:S(2)}) collective-permute-start(bf16[8,4096]{1,0:T(8,128)(2,1)S(1)} %collective-permute-done.26), channel_id=1, source_target_pairs={{0,2},{2,4},{4,6},{6,8},{8,10},{10,12},{12,14},{14,16},{16,18},{18... | collective-permute-start | bytes 196616 | tf_op jit(solution)/shard_map/ppermute | solution.py:32
  82.6 4.9 %collective-permute-start.30 = (bf16[8,4096]{1,0:T(8,128)(2,1)S(1)}, bf16[8,4096]{1,0:T(8,128)(2,1)S(1)}, u32[]{:S(2)}, u32[]{:S(2)}) collective-permute-start(bf16[8,4096]{1,0:T(8,128)(2,1)S(1)} %collective-permute-done.26), channel_id=1, source_target_pairs={{0,4},{2,6},{4,8},{6,10},{8,12},{10,14},{12,16},{14,18},{16,20},{1... | collective-permute-start | bytes 196616 | tf_op jit(solution)/shard_map/ppermute | solution.py:32
  84.2 5.7 %collective-permute-start.31 = (bf16[8,4096]{1,0:T(8,128)(2,1)S(1)}, bf16[8,4096]{1,0:T(8,128)(2,1)S(1)}, u32[]{:S(2)}, u32[]{:S(2)}) collective-permute-start(bf16[8,4096]{1,0:T(8,128)(2,1)S(1)} %collective-permute-done.29), channel_id=1, source_target_pairs={{0,2},{2,4},{4,6},{6,8},{8,10},{10,12},{12,14},{14,16},{16,18},{18... | collective-permute-start | bytes 196616 | tf_op jit(solution)/shard_map/ppermute | solution.py:32
  84.4 6.8 %collective-permute-start.33 = (bf16[8,4096]{1,0:T(8,128)(2,1)S(1)}, bf16[8,4096]{1,0:T(8,128)(2,1)S(1)}, u32[]{:S(2)}, u32[]{:S(2)}) collective-permute-start(bf16[8,4096]{1,0:T(8,128)(2,1)S(1)} %collective-permute-done.29), channel_id=1, source_target_pairs={{0,4},{2,6},{4,8},{6,10},{8,12},{10,14},{12,16},{14,18},{16,20},{1... | collective-permute-start | bytes 196616 | tf_op jit(solution)/shard_map/ppermute | solution.py:32
  91.2 7.9 %collective-permute-start.34 = (bf16[64,4096]{1,0:T(8,128)(2,1)S(1)}, bf16[64,4096]{1,0:T(8,128)(2,1)S(1)}, u32[]{:S(2)}, u32[]{:S(2)}) collective-permute-start(bf16[64,4096]{1,0:T(8,128)(2,1)S(1)} %constant_dynamic-update-slice_fusion.24.refs_0_), channel_id=1, source_target_pairs={{0,1},{1,0},{2,3},{3,2},{4,5},{5,4},{6,7},{7,6},{8,9},{9,8},{10,11... | collective-permute-start | bytes 1572872 | tf_op jit(solution)/shard_map/ppermute | solution.py:45
  (4 other events, 14.4 us)

commit v3 on v2

--- a/solution.py
+++ b/solution.py
@@ -37,13 +37,13 @@
     for distance in range(0, far, 2):
         last = distance + 2 == far
         onward = [along(value, 2) for value in (carried[:1] if last else carried)]
-        held += [along(value, 1) for value in carried]
+        held += [along(jnp.concatenate(carried, axis=0), 1)]
         held += onward
         carried = onward
-    cuts = (0, chips // 2, 3 * chips // 4, chips)
+    cuts = (0, 3 * chips // 8, 9 * chips // 16)
     halves = [jnp.concatenate(held[low:high], axis=0) for low, high in zip(cuts, cuts[1:])]
     blocks = [block for half in halves for block in (half, lax.ppermute(half, axis, turn))]
-    return blocks[:-2], blocks[-2:]
+    return blocks, held[cuts[-1] :], lambda half: (half, lax.ppermute(half, axis, turn))
 
 
 def split3(value):
@@ -204,8 +204,9 @@
     out_proj = project(out_grads, out_signs).reshape(local_count, length, -1)
     outer = jnp.einsum("sti,stj->sij", in_proj, out_proj, precision=lax.Precision.HIGHEST)
     per_sample = outer.reshape(local_count, -1).astype(jnp.bfloat16)
-    first, last = gather_samples(per_sample, "dp")
-    rows, gram = early(first)
+    first, pieces, exchange = gather_samples(per_sample, "dp")
+    rows, gram, *pieces[-2:] = lax.optimization_barrier((*early(first), *pieces[-2:]))
+    last = exchange(jnp.concatenate(pieces, axis=0))
     own_rows = per_sample.shape[1] // lax.axis_size("dp")
     place = lax.axis_index("dp").astype(jnp.int32).reshape(1)
     return tail(place, rows, gram, last, local_count, own_rows)

time: 116 us -> 116 us (level)
  starting transfers between devices: 80.3 us -> 74.4 us
  local copies, waits for them, and re-layouts: 0.64 us -> 6.33 us
    ppermute x31 -> x23, starting transfers between devices: 68.4 us -> 46.6 us  [along(): return lax.ppermute(value, axis, pairs)]
    ppermute x1, starting transfers between devices: 0.01 us -> 20.5 us  [gather_samples(): carried = [own, lax.ppermute(own, axis, turn)]]
    unnamed x31 -> x27, local copies, waits for them, and re-layouts: 0.18 us -> 5.24 us
    ppermute x3, starting transfers between devices: 11.8 us -> 7.32 us  [gather_samples(): lax.ppermute(half, axis, turn)]
    ppermute x31 -> x23, waiting for transfers between devices: 4.93 us -> 2.45 us  [along(): return lax.ppermute(value, axis, pairs)]
    pallas_call x1, Pallas kernels: 15.1 us -> 17.4 us  [tail(): pl.pallas_call(tail_kernel, name='fisher_and_solve', out_shape=(jax.Shape...]
    ppermute x3, waiting for transfers between devices: 0.01 us -> 1.88 us  [gather_samples(): lax.ppermute(half, axis, turn)]
    pallas_call x1, Pallas kernels: 3.05 us -> 1.81 us  [early(): pl.pallas_call(early_kernel, name='early_gram', out_shape=(jax.ShapeDtype...]
  transfers between devices with their start and end apart: 35 -> 27, of which waited for: 6 -> 3; matrix products, arithmetic and copies ran while one was open for 0% -> 2% of each run, Pallas kernels for 3% -> 2%
where the time goes in v3:
time: 116 us; the launch traced here: 115 us
  starting transfers between devices  74.4 us (64%)
  Pallas kernels  19.2 us (17%)
  matrix products  8.58 us (7%)
  local copies, waits for them, and re-layouts  6.33 us (5%)
  waiting for transfers between devices  4.33 us (4%)
    ppermute x23, starting transfers between devices, along(): return lax.ppermute(value, axis, pairs)  46.6 us
    ppermute x1, starting transfers between devices, gather_samples(): carried = [own, lax.ppermute(own, axis, turn)]  20.5 us
    pallas_call x1, Pallas kernels, tail(): pl.pallas_call(tail_kernel, name='fisher_and_solve', out_shape=(jax.Shape...  17.4 us
    dot_general x2, matrix products, project(): lax.dot_general(flat_rows, sign_table, (((1,), (1,)), ((), ())), preferre...  7.95 us
    ppermute x3, starting transfers between devices, gather_samples(): lax.ppermute(half, axis, turn)  7.32 us
    unnamed x27, local copies, waits for them, and re-layouts  5.24 us
    ppermute x23, waiting for transfers between devices, along(): return lax.ppermute(value, axis, pairs)  2.45 us
  transfers between devices with their start and end apart: 27, of which 3 were waited for; matrix products, arithmetic and copies ran while one was open for 2% of the time, Pallas kernels for 2%

profile of v3, /device:TPU:37, one launch (start us, length us, event | category | flops | bytes accessed | tf_op | source)
XLA Modules:
  0.0 114.5 jit_solution(3437681743644614941)
XLA Ops:
  1.4 4.4 %fusion.1 = f32[256,64]{0,1:T(8,128)S(1)} fusion(bf16[256,8192]{1,0:T(8,128)(2,1)} %bitcast.14, s32[64,8192]{1,0:T(8,128)} %param.8, f32[256]{0:T(256)S(1)} %mul.33), kind=kOutput, calls=%fused_computation.6 | convolution fusion | flops 270024704 | bytes 6358016 | tf_op jit(solution)/shard_map/dot_general | solution.py:19
  5.9 3.6 %fusion = f32[256,64]{0,1:T(8,128)S(1)} fusion(bf16[256,8192]{1,0:T(8,128)(2,1)} %bitcast.13, s32[64,8192]{1,0:T(8,128)S(1)} %copy-done.2), kind=kOutput, calls=%fused_computation.4 | convolution fusion | flops 270024704 | bytes 6356992 | tf_op jit(solution)/shard_map/dot_general | solution.py:19
  10.4 20.5 %collective-permute-start = (bf16[8,4096]{1,0:T(8,128)(2,1)S(1)}, bf16[8,4096]{1,0:T(8,128)(2,1)S(1)}, u32[]{:S(2)}, u32[]{:S(2)}) collective-permute-start(bf16[8,4096]{1,0:T(8,128)(2,1)S(1)} %convert_element_type.16), channel_id=1, source_target_pairs={{0,1},{1,0},{2,3},{3,2},{4,5},{5,4},{6,7},{7,6},{8,9},{9,8},{10,11... | collective-permute-start | bytes 196616 | tf_op jit(solution)/shard_map/ppermute | solution.py:34
  30.9 4.0 %collective-permute-start.2 = (bf16[8,4096]{1,0:T(8,128)(2,1)S(1)}, bf16[8,4096]{1,0:T(8,128)(2,1)S(1)}, u32[]{:S(2)}, u32[]{:S(2)}) collective-permute-start(bf16[8,4096]{1,0:T(8,128)(2,1)S(1)} %convert_element_type.16), channel_id=1, source_target_pairs={{0,4},{2,6},{4,8},{6,10},{8,12},{10,14},{12,16},{14,18},{16,20},{1... | collective-permute-start | bytes 196616 | tf_op jit(solution)/shard_map/ppermute | solution.py:32
  34.9 0.9 collective-permute-start.3
  35.8 1.8 %collective-permute-start.1 = (bf16[16,4096]{1,0:T(8,128)(2,1)S(1)}, bf16[16,4096]{1,0:T(8,128)(2,1)S(1)}, u32[]{:S(2)}, u32[]{:S(2)}) collective-permute-start(bf16[16,4096]{1,0:T(8,128)(2,1)S(1)} %pad_maximum_fusion), channel_id=1, source_target_pairs={{0,2},{2,4},{4,6},{6,8},{8,10},{10,12},{12,14},{14,16},{16,18},{18... | collective-permute-start | bytes 393224 | tf_op jit(solution)/shard_map/ppermute | solution.py:32
  37.7 2.5 %collective-permute-start.5 = (bf16[8,4096]{1,0:T(8,128)(2,1)S(1)}, bf16[8,4096]{1,0:T(8,128)(2,1)S(1)}, u32[]{:S(2)}, u32[]{:S(2)}) collective-permute-start(bf16[8,4096]{1,0:T(8,128)(2,1)S(1)} %collective-permute-done.2), channel_id=1, source_target_pairs={{0,4},{2,6},{4,8},{6,10},{8,12},{10,14},{12,16},{14,18},{16,20},{1... | collective-permute-start | bytes 196616 | tf_op jit(solution)/shard_map/ppermute | solution.py:32
  40.2 2.1 %collective-permute-start.6 = (bf16[8,4096]{1,0:T(8,128)(2,1)S(1)}, bf16[8,4096]{1,0:T(8,128)(2,1)S(1)}, u32[]{:S(2)}, u32[]{:S(2)}) collective-permute-start(bf16[8,4096]{1,0:T(8,128)(2,1)S(1)} %collective-permute-done.3), channel_id=1, source_target_pairs={{0,4},{2,6},{4,8},{6,10},{8,12},{10,14},{12,16},{14,18},{16,20},{1... | collective-permute-start | bytes 196616 | tf_op jit(solution)/shard_map/ppermute | solution.py:32
  43.0 2.5 %collective-permute-start.8 = (bf16[8,4096]{1,0:T(8,128)(2,1)S(1)}, bf16[8,4096]{1,0:T(8,128)(2,1)S(1)}, u32[]{:S(2)}, u32[]{:S(2)}) collective-permute-start(bf16[8,4096]{1,0:T(8,128)(2,1)S(1)} %collective-permute-done.5), channel_id=1, source_target_pairs={{0,4},{2,6},{4,8},{6,10},{8,12},{10,14},{12,16},{14,18},{16,20},{1... | collective-permute-start | bytes 196616 | tf_op jit(solution)/shard_map/ppermute | solution.py:32
  45.5 1.7 %collective-permute-start.7 = (bf16[16,4096]{1,0:T(8,128)(2,1)S(1)}, bf16[16,4096]{1,0:T(8,128)(2,1)S(1)}, u32[]{:S(2)}, u32[]{:S(2)}) collective-permute-start(bf16[16,4096]{1,0:T(8,128)(2,1)S(1)} %pad_maximum_fusion.2), channel_id=1, source_target_pairs={{0,2},{2,4},{4,6},{6,8},{8,10},{10,12},{12,14},{14,16},{16,18},{18... | collective-permute-start | bytes 393224 | tf_op jit(solution)/shard_map/ppermute | solution.py:32
  47.2 1.1 collective-permute-start.9
  48.3 2.4 %collective-permute-start.11 = (bf16[8,4096]{1,0:T(8,128)(2,1)S(1)}, bf16[8,4096]{1,0:T(8,128)(2,1)S(1)}, u32[]{:S(2)}, u32[]{:S(2)}) collective-permute-start(bf16[8,4096]{1,0:T(8,128)(2,1)S(1)} %collective-permute-done.8), channel_id=1, source_target_pairs={{0,4},{2,6},{4,8},{6,10},{8,12},{10,14},{12,16},{14,18},{16,20},{1... | collective-permute-start | bytes 196616 | tf_op jit(solution)/shard_map/ppermute | solution.py:32
  50.7 1.5 %collective-permute-done.9 = bf16[8,4096]{1,0:T(8,128)(2,1)S(1)} collective-permute-done((bf16[8,4096]{1,0:T(8,128)(2,1)S(1)}, bf16[8,4096]{1,0:T(8,128)(2,1)S(1)}, u32[]{:S(2)}, u32[]{:S(2)}) %collective-permute-start.9) | collective-permute-done | bytes 65568 | tf_op jit(solution)/shard_map/ppermute | solution.py:32
  52.2 1.8 %collective-permute-start.10 = (bf16[16,4096]{1,0:T(8,128)(2,1)S(1)}, bf16[16,4096]{1,0:T(8,128)(2,1)S(1)}, u32[]{:S(2)}, u32[]{:S(2)}) collective-permute-start(bf16[16,4096]{1,0:T(8,128)(2,1)S(1)} %pad_maximum_fusion.3), channel_id=1, source_target_pairs={{0,2},{2,4},{4,6},{6,8},{8,10},{10,12},{12,14},{14,16},{16,18},{18... | collective-permute-start | bytes 393224 | tf_op jit(solution)/shard_map/ppermute | solution.py:32
  54.5 2.7 %collective-permute-start.15 = (bf16[8,4096]{1,0:T(8,128)(2,1)S(1)}, bf16[8,4096]{1,0:T(8,128)(2,1)S(1)}, u32[]{:S(2)}, u32[]{:S(2)}) collective-permute-start(bf16[8,4096]{1,0:T(8,128)(2,1)S(1)} %collective-permute-done.11), channel_id=1, source_target_pairs={{0,4},{2,6},{4,8},{6,10},{8,12},{10,14},{12,16},{14,18},{16,20},{1... | collective-permute-start | bytes 196616 | tf_op jit(solution)/shard_map/ppermute | solution.py:32
  57.2 0.9 collective-permute-done.13
  58.1 1.9 %collective-permute-start.14 = (bf16[16,4096]{1,0:T(8,128)(2,1)S(1)}, bf16[16,4096]{1,0:T(8,128)(2,1)S(1)}, u32[]{:S(2)}, u32[]{:S(2)}) collective-permute-start(bf16[16,4096]{1,0:T(8,128)(2,1)S(1)} %pad_maximum_fusion.4), channel_id=1, source_target_pairs={{0,2},{2,4},{4,6},{6,8},{8,10},{10,12},{12,14},{14,16},{16,18},{18... | collective-permute-start | bytes 393224 | tf_op jit(solution)/shard_map/ppermute | solution.py:32
  60.1 1.6 %collective-permute-start.16 = (bf16[8,4096]{1,0:T(8,128)(2,1)S(1)}, bf16[8,4096]{1,0:T(8,128)(2,1)S(1)}, u32[]{:S(2)}, u32[]{:S(2)}) collective-permute-start(bf16[8,4096]{1,0:T(8,128)(2,1)S(1)} %collective-permute-done.13), channel_id=1, source_target_pairs={{0,4},{2,6},{4,8},{6,10},{8,12},{10,14},{12,16},{14,18},{16,20},{1... | collective-permute-start | bytes 196616 | tf_op jit(solution)/shard_map/ppermute | solution.py:32
  61.7 1.3 %collective-permute-start.18 = (bf16[8,4096]{1,0:T(8,128)(2,1)S(1)}, bf16[8,4096]{1,0:T(8,128)(2,1)S(1)}, u32[]{:S(2)}, u32[]{:S(2)}) collective-permute-start(bf16[8,4096]{1,0:T(8,128)(2,1)S(1)} %collective-permute-done.15), channel_id=1, source_target_pairs={{0,4},{2,6},{4,8},{6,10},{8,12},{10,14},{12,16},{14,18},{16,20},{1... | collective-permute-start | bytes 196616 | tf_op jit(solution)/shard_map/ppermute | solution.py:32
  63.0 3.4 %collective-permute-start.12 = (bf16[128,4096]{1,0:T(8,128)(2,1)S(1)}, bf16[128,4096]{1,0:T(8,128)(2,1)S(1)}, u32[]{:S(2)}, u32[]{:S(2)}) collective-permute-start(bf16[128,4096]{1,0:T(8,128)(2,1)S(1)} %constant_dynamic-update-slice_fusion.refs_0_), channel_id=1, source_target_pairs={{0,1},{1,0},{2,3},{3,2},{4,5},{5,4},{6,7},{7,6},{8,9},{9,8},{10,11... | collective-permute-start | bytes 3145736 | tf_op jit(solution)/shard_map/ppermute | solution.py:45
  66.4 3.8 %collective-permute-start.21 = (bf16[8,4096]{1,0:T(8,128)(2,1)S(1)}, bf16[8,4096]{1,0:T(8,128)(2,1)S(1)}, u32[]{:S(2)}, u32[]{:S(2)}) collective-permute-start(bf16[8,4096]{1,0:T(8,128)(2,1)S(1)} %collective-permute-done.16), channel_id=1, source_target_pairs={{0,4},{2,6},{4,8},{6,10},{8,12},{10,14},{12,16},{14,18},{16,20},{1... | collective-permute-start | bytes 196616 | tf_op jit(solution)/shard_map/ppermute | solution.py:32
  70.3 1.4 %collective-permute-start.17 = (bf16[16,4096]{1,0:T(8,128)(2,1)S(1)}, bf16[16,4096]{1,0:T(8,128)(2,1)S(1)}, u32[]{:S(2)}, u32[]{:S(2)}) collective-permute-start(bf16[16,4096]{1,0:T(8,128)(2,1)S(1)} %pad_maximum_fusion.5), channel_id=1, source_target_pairs={{0,2},{2,4},{4,6},{6,8},{8,10},{10,12},{12,14},{14,16},{16,18},{18... | collective-permute-start | bytes 393224 | tf_op jit(solution)/shard_map/ppermute | solution.py:32
  71.7 2.9 %collective-permute-start.20 = (bf16[8,4096]{1,0:T(8,128)(2,1)S(1)}, bf16[8,4096]{1,0:T(8,128)(2,1)S(1)}, u32[]{:S(2)}, u32[]{:S(2)}) collective-permute-start(bf16[8,4096]{1,0:T(8,128)(2,1)S(1)} %collective-permute-done.18), channel_id=1, source_target_pairs={{0,4},{2,6},{4,8},{6,10},{8,12},{10,14},{12,16},{14,18},{16,20},{1... | collective-permute-start | bytes 196616 | tf_op jit(solution)/shard_map/ppermute | solution.py:32
  75.5 1.9 %collective-permute-start.22 = (bf16[8,4096]{1,0:T(8,128)(2,1)S(1)}, bf16[8,4096]{1,0:T(8,128)(2,1)S(1)}, u32[]{:S(2)}, u32[]{:S(2)}) collective-permute-start(bf16[8,4096]{1,0:T(8,128)(2,1)S(1)} %collective-permute-done.21), channel_id=1, source_target_pairs={{0,4},{2,6},{4,8},{6,10},{8,12},{10,14},{12,16},{14,18},{16,20},{1... | collective-permute-start | bytes 196616 | tf_op jit(solution)/shard_map/ppermute | solution.py:32
  77.5 3.8 %collective-permute-start.24 = (bf16[8,4096]{1,0:T(8,128)(2,1)S(1)}, bf16[8,4096]{1,0:T(8,128)(2,1)S(1)}, u32[]{:S(2)}, u32[]{:S(2)}) collective-permute-start(bf16[8,4096]{1,0:T(8,128)(2,1)S(1)} %collective-permute-done.20), channel_id=1, source_target_pairs={{0,4},{2,6},{4,8},{6,10},{8,12},{10,14},{12,16},{14,18},{16,20},{1... | collective-permute-start | bytes 196616 | tf_op jit(solution)/shard_map/ppermute | solution.py:32
  81.5 3.0 %collective-permute-start.23 = (bf16[16,4096]{1,0:T(8,128)(2,1)S(1)}, bf16[16,4096]{1,0:T(8,128)(2,1)S(1)}, u32[]{:S(2)}, u32[]{:S(2)}) collective-permute-start(bf16[16,4096]{1,0:T(8,128)(2,1)S(1)} %pad_maximum_fusion.6), channel_id=1, source_target_pairs={{0,2},{2,4},{4,6},{6,8},{8,10},{10,12},{12,14},{14,16},{16,18},{18... | collective-permute-start | bytes 393224 | tf_op jit(solution)/shard_map/ppermute | solution.py:32
  86.5 1.8 %early_gram.1 = (bf16[384,4096]{1,0:T(8,128)(2,1)S(1)}, f32[384,384]{1,0:T(8,128)S(1)}) custom-call(bf16[128,4096]{1,0:T(8,128)(2,1)S(1)} %constant_dynamic-update-slice_fusion.refs_0_, bf16[128,4096]{1,0:T(8,128)(2,1)S(1)} %collective-permute-done.12.refs_1_, bf16[64,4096]{1,0:T(8,128)(2,1)S(1)} %constant_dynamic-update-slice_fusion.12.refs_2_, ...), custom_call_target="tpu_custom_call" | custom-call | flops 1207959552 | bytes 6291456 | tf_op jit(solution)/shard_map/early_gram/pallas_call | solution.py:84
  88.3 0.8 copy-done
  90.4 3.7 %collective-permute-start.26 = (bf16[64,4096]{1,0:T(8,128)(2,1)}, bf16[64,4096]{1,0:T(8,128)(2,1)}, u32[]{:S(2)}, u32[]{:S(2)}) collective-permute-start(bf16[64,4096]{1,0:T(8,128)(2,1)} %constant_dynamic-update-slice_fusion.18.refs_0_), channel_id=1, source_target_pairs={{0,1},{1,0},{2,3},{3,2},{4,5},{5,4},{6,7},{7,6},{8,9},{9,8},{10,11... | collective-permute-start | bytes 1572872 | tf_op jit(solution)/shard_map/ppermute | solution.py:46
  94.2 1.9 %collective-permute-done.26.refs_1_ = bf16[64,4096]{1,0:T(8,128)(2,1)} collective-permute-done((bf16[64,4096]{1,0:T(8,128)(2,1)}, bf16[64,4096]{1,0:T(8,128)(2,1)}, u32[]{:S(2)}, u32[]{:S(2)}) %collective-permute-start.26) | collective-permute-done | bytes 524320 | tf_op jit(solution)/shard_map/ppermute | solution.py:46
  96.1 1.1 copy-done.1
  97.1 17.4 %fisher_and_solve.1 = (bf16[64,4096]{1,0:T(8,128)(2,1)}, f32[8,4096]{1,0:T(8,128)}) custom-call(s32[1]{0:T(128)} %bitcast.place_ref, bf16[384,4096]{1,0:T(8,128)(2,1)S(1)} %get-tuple-element.10.first_ref, f32[384,384]{1,0:T(8,128)S(1)} %copy-done.1, bf16[64,4096]{1,0:T(8,128)(2,1)} %constant_dynamic-update-slice_fusion.18.refs_0_, ...), custom_call_target="tpu_custom_call" | custom-call | tf_op jit(solution)/shard_map/fisher_and_solve/pallas_call | solution.py:181
  (70 shorter events, 7.4 us)
Async XLA Ops:
  1.4 4.5 %copy-start.2 = (s32[64,8192]{1,0:T(8,128)S(1)}, s32[64,8192]{1,0:T(8,128)}, u32[]{:S(2)}) copy-start(s32[64,8192]{1,0:T(8,128)} %param.9) | copy-start | bytes 6291460
  10.4 24.6 %collective-permute-start = (bf16[8,4096]{1,0:T(8,128)(2,1)S(1)}, bf16[8,4096]{1,0:T(8,128)(2,1)S(1)}, u32[]{:S(2)}, u32[]{:S(2)}) collective-permute-start(bf16[8,4096]{1,0:T(8,128)(2,1)S(1)} %convert_element_type.16), channel_id=1, source_target_pairs={{0,1},{1,0},{2,3},{3,2},{4,5},{5,4},{6,7},{7,6},{8,9},{9,8},{10,11... | collective-permute-start | bytes 196616 | tf_op jit(solution)/shard_map/ppermute | solution.py:34
  30.9 6.8 %collective-permute-start.2 = (bf16[8,4096]{1,0:T(8,128)(2,1)S(1)}, bf16[8,4096]{1,0:T(8,128)(2,1)S(1)}, u32[]{:S(2)}, u32[]{:S(2)}) collective-permute-start(bf16[8,4096]{1,0:T(8,128)(2,1)S(1)} %convert_element_type.16), channel_id=1, source_target_pairs={{0,4},{2,6},{4,8},{6,10},{8,12},{10,14},{12,16},{14,18},{16,20},{1... | collective-permute-start | bytes 196616 | tf_op jit(solution)/shard_map/ppermute | solution.py:32
  34.9 5.3 %collective-permute-start.3 = (bf16[8,4096]{1,0:T(8,128)(2,1)S(1)}, bf16[8,4096]{1,0:T(8,128)(2,1)S(1)}, u32[]{:S(2)}, u32[]{:S(2)}) collective-permute-start(bf16[8,4096]{1,0:T(8,128)(2,1)S(1)} %collective-permute-done), channel_id=1, source_target_pairs={{0,4},{2,6},{4,8},{6,10},{8,12},{10,14},{12,16},{14,18},{16,20},{1... | collective-permute-start | bytes 196616 | tf_op jit(solution)/shard_map/ppermute | solution.py:32
  35.8 12.4 %collective-permute-start.1 = (bf16[16,4096]{1,0:T(8,128)(2,1)S(1)}, bf16[16,4096]{1,0:T(8,128)(2,1)S(1)}, u32[]{:S(2)}, u32[]{:S(2)}) collective-permute-start(bf16[16,4096]{1,0:T(8,128)(2,1)S(1)} %pad_maximum_fusion), channel_id=1, source_target_pairs={{0,2},{2,4},{4,6},{6,8},{8,10},{10,12},{12,14},{14,16},{16,18},{18... | collective-permute-start | bytes 393224 | tf_op jit(solution)/shard_map/ppermute | solution.py:32
  37.7 5.3 %collective-permute-start.5 = (bf16[8,4096]{1,0:T(8,128)(2,1)S(1)}, bf16[8,4096]{1,0:T(8,128)(2,1)S(1)}, u32[]{:S(2)}, u32[]{:S(2)}) collective-permute-start(bf16[8,4096]{1,0:T(8,128)(2,1)S(1)} %collective-permute-done.2), channel_id=1, source_target_pairs={{0,4},{2,6},{4,8},{6,10},{8,12},{10,14},{12,16},{14,18},{16,20},{1... | collective-permute-start | bytes 196616 | tf_op jit(solution)/shard_map/ppermute | solution.py:32
  40.2 5.3 %collective-permute-start.6 = (bf16[8,4096]{1,0:T(8,128)(2,1)S(1)}, bf16[8,4096]{1,0:T(8,128)(2,1)S(1)}, u32[]{:S(2)}, u32[]{:S(2)}) collective-permute-start(bf16[8,4096]{1,0:T(8,128)(2,1)S(1)} %collective-permute-done.3), channel_id=1, source_target_pairs={{0,4},{2,6},{4,8},{6,10},{8,12},{10,14},{12,16},{14,18},{16,20},{1... | collective-permute-start | bytes 196616 | tf_op jit(solution)/shard_map/ppermute | solution.py:32
  42.3 12.1 %collective-permute-start.4 = (bf16[16,4096]{1,0:T(8,128)(2,1)S(1)}, bf16[16,4096]{1,0:T(8,128)(2,1)S(1)}, u32[]{:S(2)}, u32[]{:S(2)}) collective-permute-start(bf16[16,4096]{1,0:T(8,128)(2,1)S(1)} %pad_maximum_fusion.1), channel_id=1, source_target_pairs={{0,2},{2,4},{4,6},{6,8},{8,10},{10,12},{12,14},{14,16},{16,18},{18... | collective-permute-start | bytes 393224 | tf_op jit(solution)/shard_map/ppermute | solution.py:32
  43.0 5.3 %collective-permute-start.8 = (bf16[8,4096]{1,0:T(8,128)(2,1)S(1)}, bf16[8,4096]{1,0:T(8,128)(2,1)S(1)}, u32[]{:S(2)}, u32[]{:S(2)}) collective-permute-start(bf16[8,4096]{1,0:T(8,128)(2,1)S(1)} %collective-permute-done.5), channel_id=1, source_target_pairs={{0,4},{2,6},{4,8},{6,10},{8,12},{10,14},{12,16},{14,18},{16,20},{1... | collective-permute-start | bytes 196616 | tf_op jit(solution)/shard_map/ppermute | solution.py:32
  45.5 16.1 %collective-permute-start.7 = (bf16[16,4096]{1,0:T(8,128)(2,1)S(1)}, bf16[16,4096]{1,0:T(8,128)(2,1)S(1)}, u32[]{:S(2)}, u32[]{:S(2)}) collective-permute-start(bf16[16,4096]{1,0:T(8,128)(2,1)S(1)} %pad_maximum_fusion.2), channel_id=1, source_target_pairs={{0,2},{2,4},{4,6},{6,8},{8,10},{10,12},{12,14},{14,16},{16,18},{18... | collective-permute-start | bytes 393224 | tf_op jit(solution)/shard_map/ppermute | solution.py:32
  47.2 5.0 %collective-permute-start.9 = (bf16[8,4096]{1,0:T(8,128)(2,1)S(1)}, bf16[8,4096]{1,0:T(8,128)(2,1)S(1)}, u32[]{:S(2)}, u32[]{:S(2)}) collective-permute-start(bf16[8,4096]{1,0:T(8,128)(2,1)S(1)} %collective-permute-done.6), channel_id=1, source_target_pairs={{0,4},{2,6},{4,8},{6,10},{8,12},{10,14},{12,16},{14,18},{16,20},{1... | collective-permute-start | bytes 196616 | tf_op jit(solution)/shard_map/ppermute | solution.py:32
  48.3 6.2 %collective-permute-start.11 = (bf16[8,4096]{1,0:T(8,128)(2,1)S(1)}, bf16[8,4096]{1,0:T(8,128)(2,1)S(1)}, u32[]{:S(2)}, u32[]{:S(2)}) collective-permute-start(bf16[8,4096]{1,0:T(8,128)(2,1)S(1)} %collective-permute-done.8), channel_id=1, source_target_pairs={{0,4},{2,6},{4,8},{6,10},{8,12},{10,14},{12,16},{14,18},{16,20},{1... | collective-permute-start | bytes 196616 | tf_op jit(solution)/shard_map/ppermute | solution.py:32
  52.2 10.7 %collective-permute-start.10 = (bf16[16,4096]{1,0:T(8,128)(2,1)S(1)}, bf16[16,4096]{1,0:T(8,128)(2,1)S(1)}, u32[]{:S(2)}, u32[]{:S(2)}) collective-permute-start(bf16[16,4096]{1,0:T(8,128)(2,1)S(1)} %pad_maximum_fusion.3), channel_id=1, source_target_pairs={{0,2},{2,4},{4,6},{6,8},{8,10},{10,12},{12,14},{14,16},{16,18},{18... | collective-permute-start | bytes 393224 | tf_op jit(solution)/shard_map/ppermute | solution.py:32
  54.0 4.1 %collective-permute-start.13 = (bf16[8,4096]{1,0:T(8,128)(2,1)S(1)}, bf16[8,4096]{1,0:T(8,128)(2,1)S(1)}, u32[]{:S(2)}, u32[]{:S(2)}) collective-permute-start(bf16[8,4096]{1,0:T(8,128)(2,1)S(1)} %collective-permute-done.9), channel_id=1, source_target_pairs={{0,4},{2,6},{4,8},{6,10},{8,12},{10,14},{12,16},{14,18},{16,20},{1... | collective-permute-start | bytes 196616 | tf_op jit(solution)/shard_map/ppermute | solution.py:32
  54.5 7.2 %collective-permute-start.15 = (bf16[8,4096]{1,0:T(8,128)(2,1)S(1)}, bf16[8,4096]{1,0:T(8,128)(2,1)S(1)}, u32[]{:S(2)}, u32[]{:S(2)}) collective-permute-start(bf16[8,4096]{1,0:T(8,128)(2,1)S(1)} %collective-permute-done.11), channel_id=1, source_target_pairs={{0,4},{2,6},{4,8},{6,10},{8,12},{10,14},{12,16},{14,18},{16,20},{1... | collective-permute-start | bytes 196616 | tf_op jit(solution)/shard_map/ppermute | solution.py:32
  58.1 17.4 %collective-permute-start.14 = (bf16[16,4096]{1,0:T(8,128)(2,1)S(1)}, bf16[16,4096]{1,0:T(8,128)(2,1)S(1)}, u32[]{:S(2)}, u32[]{:S(2)}) collective-permute-start(bf16[16,4096]{1,0:T(8,128)(2,1)S(1)} %pad_maximum_fusion.4), channel_id=1, source_target_pairs={{0,2},{2,4},{4,6},{6,8},{8,10},{10,12},{12,14},{14,16},{16,18},{18... | collective-permute-start | bytes 393224 | tf_op jit(solution)/shard_map/ppermute | solution.py:32
  60.1 6.4 %collective-permute-start.16 = (bf16[8,4096]{1,0:T(8,128)(2,1)S(1)}, bf16[8,4096]{1,0:T(8,128)(2,1)S(1)}, u32[]{:S(2)}, u32[]{:S(2)}) collective-permute-start(bf16[8,4096]{1,0:T(8,128)(2,1)S(1)} %collective-permute-done.13), channel_id=1, source_target_pairs={{0,4},{2,6},{4,8},{6,10},{8,12},{10,14},{12,16},{14,18},{16,20},{1... | collective-permute-start | bytes 196616 | tf_op jit(solution)/shard_map/ppermute | solution.py:32
  61.7 10.0 %collective-permute-start.18 = (bf16[8,4096]{1,0:T(8,128)(2,1)S(1)}, bf16[8,4096]{1,0:T(8,128)(2,1)S(1)}, u32[]{:S(2)}, u32[]{:S(2)}) collective-permute-start(bf16[8,4096]{1,0:T(8,128)(2,1)S(1)} %collective-permute-done.15), channel_id=1, source_target_pairs={{0,4},{2,6},{4,8},{6,10},{8,12},{10,14},{12,16},{14,18},{16,20},{1... | collective-permute-start | bytes 196616 | tf_op jit(solution)/shard_map/ppermute | solution.py:32
  63.0 23.5 %collective-permute-start.12 = (bf16[128,4096]{1,0:T(8,128)(2,1)S(1)}, bf16[128,4096]{1,0:T(8,128)(2,1)S(1)}, u32[]{:S(2)}, u32[]{:S(2)}) collective-permute-start(bf16[128,4096]{1,0:T(8,128)(2,1)S(1)} %constant_dynamic-update-slice_fusion.refs_0_), channel_id=1, source_target_pairs={{0,1},{1,0},{2,3},{3,2},{4,5},{5,4},{6,7},{7,6},{8,9},{9,8},{10,11... | collective-permute-start | bytes 3145736 | tf_op jit(solution)/shard_map/ppermute | solution.py:45
  66.4 8.2 %collective-permute-start.21 = (bf16[8,4096]{1,0:T(8,128)(2,1)S(1)}, bf16[8,4096]{1,0:T(8,128)(2,1)S(1)}, u32[]{:S(2)}, u32[]{:S(2)}) collective-permute-start(bf16[8,4096]{1,0:T(8,128)(2,1)S(1)} %collective-permute-done.16), channel_id=1, source_target_pairs={{0,4},{2,6},{4,8},{6,10},{8,12},{10,14},{12,16},{14,18},{16,20},{1... | collective-permute-start | bytes 196616 | tf_op jit(solution)/shard_map/ppermute | solution.py:32
  70.3 11.0 %collective-permute-start.17 = (bf16[16,4096]{1,0:T(8,128)(2,1)S(1)}, bf16[16,4096]{1,0:T(8,128)(2,1)S(1)}, u32[]{:S(2)}, u32[]{:S(2)}) collective-permute-start(bf16[16,4096]{1,0:T(8,128)(2,1)S(1)} %pad_maximum_fusion.5), channel_id=1, source_target_pairs={{0,2},{2,4},{4,6},{6,8},{8,10},{10,12},{12,14},{14,16},{16,18},{18... | collective-permute-start | bytes 393224 | tf_op jit(solution)/shard_map/ppermute | solution.py:32
  71.7 5.8 %collective-permute-start.20 = (bf16[8,4096]{1,0:T(8,128)(2,1)S(1)}, bf16[8,4096]{1,0:T(8,128)(2,1)S(1)}, u32[]{:S(2)}, u32[]{:S(2)}) collective-permute-start(bf16[8,4096]{1,0:T(8,128)(2,1)S(1)} %collective-permute-done.18), channel_id=1, source_target_pairs={{0,4},{2,6},{4,8},{6,10},{8,12},{10,14},{12,16},{14,18},{16,20},{1... | collective-permute-start | bytes 196616 | tf_op jit(solution)/shard_map/ppermute | solution.py:32
  74.6 9.9 %collective-permute-start.25 = (bf16[16,4096]{1,0:T(8,128)(2,1)S(1)}, bf16[16,4096]{1,0:T(8,128)(2,1)S(1)}, u32[]{:S(2)}, u32[]{:S(2)}) collective-permute-start(bf16[16,4096]{1,0:T(8,128)(2,1)S(1)} %pad_maximum_fusion.7), channel_id=1, source_target_pairs={{0,2},{2,4},{4,6},{6,8},{8,10},{10,12},{12,14},{14,16},{16,18},{18... | collective-permute-start | bytes 393224 | tf_op jit(solution)/shard_map/ppermute | solution.py:32
  75.5 5.9 %collective-permute-start.22 = (bf16[8,4096]{1,0:T(8,128)(2,1)S(1)}, bf16[8,4096]{1,0:T(8,128)(2,1)S(1)}, u32[]{:S(2)}, u32[]{:S(2)}) collective-permute-start(bf16[8,4096]{1,0:T(8,128)(2,1)S(1)} %collective-permute-done.21), channel_id=1, source_target_pairs={{0,4},{2,6},{4,8},{6,10},{8,12},{10,14},{12,16},{14,18},{16,20},{1... | collective-permute-start | bytes 196616 | tf_op jit(solution)/shard_map/ppermute | solution.py:32
  77.5 11.7 %collective-permute-start.24 = (bf16[8,4096]{1,0:T(8,128)(2,1)S(1)}, bf16[8,4096]{1,0:T(8,128)(2,1)S(1)}, u32[]{:S(2)}, u32[]{:S(2)}) collective-permute-start(bf16[8,4096]{1,0:T(8,128)(2,1)S(1)} %collective-permute-done.20), channel_id=1, source_target_pairs={{0,4},{2,6},{4,8},{6,10},{8,12},{10,14},{12,16},{14,18},{16,20},{1... | collective-permute-start | bytes 196616 | tf_op jit(solution)/shard_map/ppermute | solution.py:32
  81.3 5.2 %collective-permute-start.19 = (bf16[64,4096]{1,0:T(8,128)(2,1)S(1)}, bf16[64,4096]{1,0:T(8,128)(2,1)S(1)}, u32[]{:S(2)}, u32[]{:S(2)}) collective-permute-start(bf16[64,4096]{1,0:T(8,128)(2,1)S(1)} %constant_dynamic-update-slice_fusion.12.refs_2_), channel_id=1, source_target_pairs={{0,1},{1,0},{2,3},{3,2},{4,5},{5,4},{6,7},{7,6},{8,9},{9,8},{10,11... | collective-permute-start | bytes 1572872 | tf_op jit(solution)/shard_map/ppermute | solution.py:45
  81.5 7.6 %collective-permute-start.23 = (bf16[16,4096]{1,0:T(8,128)(2,1)S(1)}, bf16[16,4096]{1,0:T(8,128)(2,1)S(1)}, u32[]{:S(2)}, u32[]{:S(2)}) collective-permute-start(bf16[16,4096]{1,0:T(8,128)(2,1)S(1)} %pad_maximum_fusion.6), channel_id=1, source_target_pairs={{0,2},{2,4},{4,6},{6,8},{8,10},{10,12},{12,14},{14,16},{16,18},{18... | collective-permute-start | bytes 393224 | tf_op jit(solution)/shard_map/ppermute | solution.py:32
  88.3 0.8 copy-start
  90.4 5.6 %collective-permute-start.26 = (bf16[64,4096]{1,0:T(8,128)(2,1)}, bf16[64,4096]{1,0:T(8,128)(2,1)}, u32[]{:S(2)}, u32[]{:S(2)}) collective-permute-start(bf16[64,4096]{1,0:T(8,128)(2,1)} %constant_dynamic-update-slice_fusion.18.refs_0_), channel_id=1, source_target_pairs={{0,1},{1,0},{2,3},{3,2},{4,5},{5,4},{6,7},{7,6},{8,9},{9,8},{10,11... | collective-permute-start | bytes 1572872 | tf_op jit(solution)/shard_map/ppermute | solution.py:46
  96.1 1.1 copy-start.1
